TPU v7x, 128 devices: a whole 4x4x4 slice. The times are simulated.
128 devices in a mesh: ka: 16 (over x_hi, z, core), band: 8 (over x_lo, y).
Axes of the slice: x: 4 (x_hi: 2, x_lo: 2; x = x_hi * 2 + x_lo), y: 4, z: 4, core: 2. Of those that a mesh axis runs over, the one named last changes fastest.
Arguments:
- occ_rows: bfloat16 [16, 2048, 128], P('ka', 'band'), may hold values from -0.5 to 0.5
- vir_rows: bfloat16 [16, 2048, 896], P('ka', 'band'), may hold values from -0.1875 to 0.1875
- trial_vectors: float32 [16, 2, 128, 896], P('ka', None, None, 'band'), may hold values from -6 to 6
- occ_energy: float32 [16, 128], P('ka'), may hold values from -1.2 to -0.3
- vir_energy: float32 [16, 896], P('ka', 'band'), may hold values from 0.1 to 1.5
- coulomb: bfloat16 [2048, 2048], P('band'), may hold values from -0.0625 to 0.0625
- exch_kernel: bfloat16 [16, 2048, 2048], P(None, 'band'), as said below
- minus_table: int32 [16, 16], replicated, may hold values from 0 to 15, as said below
Outputs:
- sigma_vectors: float32 [16, 2, 128, 896], P('ka', None, None, 'band')
Inputs may be any that keep to these rules, and one draw needn't show every extreme that they name: minus_table[k, q] is the k-point k - q on a group of 16 k-points: every row and every column holds each index once, and one q gives minus_table[k, q] == k for every k. Each exch_kernel[q] is symmetric.
All inputs are finite; a program needn't handle non-finite values.
Results may differ from a plain program's by a relative error of at most 0.0051.
Values may be sent and summed in bfloat16 or wider, within the bound.
A program may use at most 128 MiB of HBM per device.

v0:
```python
import jax
import jax.numpy as jnp
from jax import lax
from jax.sharding import PartitionSpec as P


def sent_to_all(array, axis):
    copies = jnp.broadcast_to(array, (lax.axis_size(axis), *array.shape))
    return lax.all_to_all(copies, axis, split_axis=0, concat_axis=0, tiled=True)


def taken_together(array, axis):
    return sent_to_all(array, axis).sum(axis=0)


def in_order(pieces, dim):
    pieces = jnp.moveaxis(pieces, 0, dim)
    dims = pieces.shape
    return pieces.reshape(*dims[:dim], dims[dim] * dims[dim + 1], *dims[dim + 2 :])


def gather_directly(array, axis, dim):
    pieces = sent_to_all(array, axis)
    return in_order(pieces, dim)


def split_up(array, dim, size):
    before, after = (array.shape[:dim], array.shape[dim + 1 :])
    return jnp.moveaxis(array.reshape(*before, size, -1, *after), dim, 0)


def summed_on_arrival(array, axis, dim):
    size = lax.axis_size(axis)
    pieces = lax.all_to_all(split_up(array, dim, size), axis, 0, 0, tiled=True)
    return jnp.sum(pieces, axis=0)


def per_device(
    occ_rows, vir_rows, trial_vectors, occ_energy, vir_energy, coulomb, exch_kernel, minus_table
):
    vectors = trial_vectors.shape[1]
    own_rows = occ_rows.shape[1]
    kpoints = lax.axis_size("ka")
    self_point = lax.axis_index("ka")
    trial_half = trial_vectors[0].astype(jnp.bfloat16)
    trial_full, vir_full = (
        lax.all_gather(trial_half, "band", axis=2, tiled=True),
        lax.all_gather(vir_rows[0], "band", axis=0, tiled=True),
    )
    auxiliary = vir_full.shape[0]
    occ_own = occ_rows[0]
    vir_own = vir_rows[0]
    mixed_rows = jnp.einsum(
        "ri,via->vra", occ_own, trial_full, preferred_element_type=jnp.float32
    ).astype(jnp.bfloat16)
    pair_block = jnp.einsum(
        "vra,na->vrn", mixed_rows, vir_full, preferred_element_type=jnp.float32
    ).astype(jnp.bfloat16)
    density_own = jnp.sum(
        mixed_rows.astype(jnp.float32) * vir_own.astype(jnp.float32)[None], axis=2
    )
    density_sum = taken_together(density_own, "ka")
    density_half = gather_directly(density_sum.astype(jnp.bfloat16), "band", 1)
    potential = jnp.einsum("vn,rn->vr", density_half, coulomb, preferred_element_type=jnp.float32)
    piece_width = auxiliary // kpoints
    kernel_cols = lax.dynamic_slice_in_dim(exch_kernel, self_point * piece_width, piece_width, 2)
    split_pairs = pair_block.reshape(vectors, own_rows, kpoints, piece_width)
    moved_pairs = jnp.take(
        lax.all_to_all(split_pairs, "ka", split_axis=2, concat_axis=2, tiled=True),
        minus_table,
        axis=2,
    )
    summed = jnp.einsum(
        "vrkqc,qrc->vrkc", moved_pairs, kernel_cols, preferred_element_type=jnp.float32
    )
    screened = lax.all_to_all(
        summed.astype(jnp.bfloat16), "ka", split_axis=2, concat_axis=2, tiled=True
    )
    screened = screened.reshape(vectors, own_rows, auxiliary)
    product = jnp.einsum("vrn,na->vra", screened, vir_full, preferred_element_type=jnp.float32)
    weights = (2.0 * potential[:, :, None] * vir_own.astype(jnp.float32)[None] - product).astype(
        jnp.bfloat16
    )
    partial_sums = jnp.einsum("ri,vra->via", occ_own, weights, preferred_element_type=jnp.float32)
    coupled = summed_on_arrival(partial_sums, "band", 2)
    energy_gaps = vir_energy[0][None, :] - occ_energy[0][:, None]
    return (energy_gaps[None] * trial_vectors[0] + coupled)[None]


def solution(mesh):
    in_specs = (
        P("ka", "band", None),
        P("ka", "band", None),
        P("ka", None, None, "band"),
        P("ka", None),
        P("ka", "band"),
        P("band", None),
        P(None, "band", None),
        P(),
    )
    out_specs = P("ka", None, None, "band")
    return jax.shard_map(
        per_device, mesh=mesh, in_specs=in_specs, out_specs=out_specs, check_vma=False
    )
```

profile of v0, /device:TPU:1, one launch (start us, length us, event | category | flops | bytes accessed | tf_op | source)
XLA Modules:
  0.0 214.4 jit_solution(1257399889311923718)
XLA Ops:
  6.5 0.7 all-gather.4.cloned.1.call-update
  7.3 1.1 bitcast_convert_fusion.1
  8.7 26.5 %all-gather = bf16[1,2,128,896]{2,3,1,0:T(8,128)(2,1)S(1)} all-gather(bf16[1,2,128,112]{2,3,1,0:T(8,128)(2,1)S(1)} %convert_element_type.33), channel_id=2, replica_groups=mesh['ka'=16,'band'=8] {'band'}, dimensions={3}, use_global_device_ids=true | all-gather | bytes 516096 | tf_op jit(solution)/shard_map/all_gather | solution.py:47
  36.3 13.4 %all-to-all-start = ((f32[16,2,256]{2,1,0:T(2,128)}), f32[16,2,256]{2,1,0:T(2,128)S(1)}, u32[]{:S(2)}, u32[]{:S(2)}) async-start(f32[16,2,256]{2,1,0:T(2,128)} %broadcast_in_dim.23), calls=%async_computation | async-start | bytes 65536 | tf_op jit(solution)/shard_map/all_to_all | solution.py:9
  49.6 13.0 %all-gather.4.cloned.1.call-done = bf16[1,2048,896]{2,1,0:T(8,128)(2,1)} async-done(((bf16[1,256,896]{2,1,0:T(8,128)(2,1)}), bf16[1,2048,896]{2,1,0:T(8,128)(2,1)}) %all-gather.4.cloned.1.call-update) | async-done | bytes 3670032 | tf_op jit(solution)/shard_map/all_gather | solution.py:48
  62.6 4.4 %fusion.7 = bf16[2,32,16,8,128]{4,3,2,1,0:T(8,128)(2,1)S(1)} fusion(bf16[2,256,896]{1,2,0:T(8,128)(2,1)S(1)} %get-tuple-element.6, bf16[1,2048,896]{2,1,0:T(8,128)(2,1)} %all-gather.4.cloned.1.call-done), kind=kOutput, calls=%fused_computation.11 | convolution fusion | flops 1880096768 | bytes 6684672 | tf_op jit(solution)/shard_map/vra,na->vrn/dot_general | solution.py:56
  67.1 1.9 copy.55
  69.0 7.5 %all-to-all-start.2 = ((bf16[2,256,16,128]{3,1,0,2:T(8,128)(2,1)}), bf16[2,256,16,128]{3,1,0,2:T(8,128)(2,1)S(1)}, u32[]{:S(2)}, u32[]{:S(2)}) async-start(bf16[2,256,16,128]{3,1,0,2:T(8,128)(2,1)} %bitcast.66), calls=%async_computation.2 | async-start | bytes 4194304 | tf_op jit(solution)/shard_map/all_to_all | solution.py:69
  76.6 2.7 %bitcast_convert_fusion = f32[256,128,16]{1,0,2:T(8,128)} fusion(bf16[16,256,2048]{2,1,0:T(8,128)(2,1)} %param.14, s32[]{:T(128)S(6)} %select_n.12), kind=kLoop, calls=%fused_computation.16 | loop fusion | flops 524288 | bytes 3145732
  79.3 25.5 %all-to-all-done.2 = bf16[2,256,16,128]{3,1,0,2:T(8,128)(2,1)S(1)} async-done(((bf16[2,256,16,128]{3,1,0,2:T(8,128)(2,1)}), bf16[2,256,16,128]{3,1,0,2:T(8,128)(2,1)S(1)}, u32[]{:S(2)}, u32[]{:S(2)}) %all-to-all-start.2) | async-done | bytes 2097184 | tf_op jit(solution)/shard_map/all_to_all | solution.py:69
  105.4 0.7 copy-done.1
  106.1 3.3 %all-to-all-start.1 = ((bf16[8,2,256]{2,1,0:T(2,128)(2,1)}), bf16[8,2,256]{2,1,0:T(2,128)(2,1)S(1)}, u32[]{:S(2)}, u32[]{:S(2)}) async-start(bf16[8,2,256]{2,1,0:T(2,128)(2,1)} %broadcast_in_dim.24), calls=%async_computation.1 | async-start | bytes 16384 | tf_op jit(solution)/shard_map/all_to_all | solution.py:9
  109.5 1.7 copy.34
  111.2 13.9 %gather_fusion = bf16[256,2,256,128]{3,2,1,0:T(8,128)(2,1)} fusion(bf16[2,256,16,128]{3,1,2,0:T(8,128)(2,1)S(1)} %copy.34, s32[1024]{0:T(1024)S(1)} %pad_clamp_fusion), kind=kCustom, calls=%fused_computation | custom fusion | bytes 67109888 | tf_op jit(solution)/shard_map/jit(_take)/gather | solution.py:68
  125.1 17.9 %multiply_reduce_fusion = bf16[256,128,2,16]{1,0,2,3:T(8,128)(2,1)S(1)} fusion(f32[256,128,16]{1,0,2:T(8,128)} %bitcast_convert_fusion, bf16[16,16,2,256,128]{4,3,2,1,0:T(8,128)(2,1)} %bitcast.65, pred[16,16]{1,0:T(8,128)(4,1)S(1)} %compare_and_fusion), kind=kLoop, calls=%fused_computation.1 | loop fusion | flops 66060288 | bytes 37748992
  143.0 2.6 %copy.47 = bf16[256,128,2,16]{0,1,2,3:T(8,128)(2,1)} copy(bf16[256,128,2,16]{1,0,2,3:T(8,128)(2,1)S(1)} %multiply_reduce_fusion) | data formatting | bytes 4194304 | tf_op jit(solution)/shard_map/vrkqc,qrc->vrkc/dot_general | solution.py:73
  145.6 6.9 %all-to-all-start.3 = ((bf16[2,256,16,128]{1,3,0,2:T(8,128)(2,1)}), bf16[2,256,16,128]{1,3,0,2:T(8,128)(2,1)S(1)}, u32[]{:S(2)}, u32[]{:S(2)}) async-start(bf16[2,256,16,128]{1,3,0,2:T(8,128)(2,1)} %bitcast.67), calls=%async_computation.3 | async-start | bytes 4194304 | tf_op jit(solution)/shard_map/all_to_all | solution.py:76
  152.9 28.0 %all-to-all-done.3 = bf16[2,256,16,128]{1,3,0,2:T(8,128)(2,1)S(1)} async-done(((bf16[2,256,16,128]{1,3,0,2:T(8,128)(2,1)}), bf16[2,256,16,128]{1,3,0,2:T(8,128)(2,1)S(1)}, u32[]{:S(2)}, u32[]{:S(2)}) %all-to-all-start.3) | async-done | bytes 2097184 | tf_op jit(solution)/shard_map/all_to_all | solution.py:76
  180.9 1.5 copy.35
  182.4 5.6 %fusion.14 = f32[2,896,128]{2,1,0:T(8,128)S(1)} fusion(bf16[2,256,2048]{1,2,0:T(8,128)(2,1)} %bitcast.68, bf16[1,2048,896]{2,1,0:T(8,128)(2,1)} %all-gather.4.cloned.1.call-done, f32[2,256]{1,0:T(2,128)S(1)} %convolution_multiply_fusion, f32[256,896]{0,1:T(8,128)} %copy-done.2, bf16[1,256,128]{2,1,0:T(8,128)(2,1)S(1)} %copy-done.4), kind=kOutput, calls=%fused_computation.14 | convolution fusion | flops 1997864960 | bytes 7669760 | tf_op jit(solution)/shard_map/ri,vra->via/dot_general | solution.py:84
  188.0 1.0 copy.56
  189.0 5.2 %all-to-all-start.4 = ((f32[8,2,128,112]{2,3,1,0:T(8,128)}), f32[8,2,128,112]{2,3,1,0:T(8,128)S(1)}, u32[]{:S(2)}, u32[]{:S(2)}) async-start(f32[8,2,128,112]{2,3,1,0:T(8,128)} %bitcast.64), calls=%async_computation.4 | async-start | bytes 1835008 | tf_op jit(solution)/shard_map/all_to_all | solution.py:34
  194.3 12.6 %all-to-all-done.4 = f32[8,2,128,112]{2,3,1,0:T(8,128)S(1)} async-done(((f32[8,2,128,112]{2,3,1,0:T(8,128)}), f32[8,2,128,112]{2,3,1,0:T(8,128)S(1)}, u32[]{:S(2)}, u32[]{:S(2)}) %all-to-all-start.4) | async-done | bytes 917536 | tf_op jit(solution)/shard_map/all_to_all | solution.py:34
  206.9 0.7 bitcast_add_fusion
  (31 shorter events, 2.7 us)
Async XLA Ops:
  6.5 146.0 %copy-start = (bf16[256,2048]{1,0:T(8,128)(2,1)S(1)}, bf16[256,2048]{1,0:T(8,128)(2,1)}, u32[]{:S(2)}) copy-start(bf16[256,2048]{1,0:T(8,128)(2,1)} %param.13) | copy-start | bytes 3145732
  6.5 2.1 copy-start.3
  6.5 28.7 %copy-start.4 = (bf16[1,256,128]{2,1,0:T(8,128)(2,1)S(1)}, bf16[1,256,128]{2,1,0:T(8,128)(2,1)}, u32[]{:S(2)}) copy-start(bf16[1,256,128]{2,1,0:T(8,128)(2,1)} %param.8) | copy-start | bytes 196612
  6.5 56.1 %all-gather.4.cloned.1.call-start = ((), (), s32[]{:S(2)}) async-start(), calls=%async_computation.5 | async-start | bytes 4128768 | tf_op jit(solution)/shard_map/all_gather | solution.py:48
  8.7 58.4 %copy-start.2 = (f32[256,896]{0,1:T(8,128)}, f32[256,896]{0,1:T(8,128)S(1)}, u32[]{:S(2)}) copy-start(f32[256,896]{0,1:T(8,128)S(1)} %copy.30) | copy-start | bytes 2752516
  36.3 32.8 %all-to-all-start = ((f32[16,2,256]{2,1,0:T(2,128)}), f32[16,2,256]{2,1,0:T(2,128)S(1)}, u32[]{:S(2)}, u32[]{:S(2)}) async-start(f32[16,2,256]{2,1,0:T(2,128)} %broadcast_in_dim.23), calls=%async_computation | async-start | bytes 65536 | tf_op jit(solution)/shard_map/all_to_all | solution.py:9
  69.0 7.5 %copy-start.5 = (s32[16,16]{1,0:T(8,128)S(1)}, s32[16,16]{1,0:T(8,128)}, u32[]{:S(2)}) copy-start(s32[16,16]{1,0:T(8,128)} %param.15) | copy-start | bytes 3076
  69.0 35.8 %all-to-all-start.2 = ((bf16[2,256,16,128]{3,1,0,2:T(8,128)(2,1)}), bf16[2,256,16,128]{3,1,0,2:T(8,128)(2,1)S(1)}, u32[]{:S(2)}, u32[]{:S(2)}) async-start(bf16[2,256,16,128]{3,1,0,2:T(8,128)(2,1)} %bitcast.66), calls=%async_computation.2 | async-start | bytes 4194304 | tf_op jit(solution)/shard_map/all_to_all | solution.py:69
  104.8 1.3 copy-start.1
  106.1 39.5 %all-to-all-start.1 = ((bf16[8,2,256]{2,1,0:T(2,128)(2,1)}), bf16[8,2,256]{2,1,0:T(2,128)(2,1)S(1)}, u32[]{:S(2)}, u32[]{:S(2)}) async-start(bf16[8,2,256]{2,1,0:T(2,128)(2,1)} %broadcast_in_dim.24), calls=%async_computation.1 | async-start | bytes 16384 | tf_op jit(solution)/shard_map/all_to_all | solution.py:9
  145.6 35.3 %all-to-all-start.3 = ((bf16[2,256,16,128]{1,3,0,2:T(8,128)(2,1)}), bf16[2,256,16,128]{1,3,0,2:T(8,128)(2,1)S(1)}, u32[]{:S(2)}, u32[]{:S(2)}) async-start(bf16[2,256,16,128]{1,3,0,2:T(8,128)(2,1)} %bitcast.67), calls=%async_computation.3 | async-start | bytes 4194304 | tf_op jit(solution)/shard_map/all_to_all | solution.py:76
  187.9 6.3 %copy-start.6 = (f32[1,128]{1,0:T(1,128)S(1)}, f32[1,128]{1,0:T(1,128)}, u32[]{:S(2)}) copy-start(f32[1,128]{1,0:T(1,128)} %param.11) | copy-start | bytes 1540
  187.9 6.3 %copy-start.7 = (f32[1,112]{1,0:T(1,128)S(1)}, f32[1,112]{1,0:T(1,128)}, u32[]{:S(2)}) copy-start(f32[1,112]{1,0:T(1,128)} %param.12) | copy-start | bytes 1348
  189.0 17.9 %all-to-all-start.4 = ((f32[8,2,128,112]{2,3,1,0:T(8,128)}), f32[8,2,128,112]{2,3,1,0:T(8,128)S(1)}, u32[]{:S(2)}, u32[]{:S(2)}) async-start(f32[8,2,128,112]{2,3,1,0:T(8,128)} %bitcast.64), calls=%async_computation.4 | async-start | bytes 1835008 | tf_op jit(solution)/shard_map/all_to_all | solution.py:34
Sparse Core Ops, SparseCore 0:
  9.0 53.6 all-gather.3
where the time goes:
time: 216 us; the launch traced here: 214 us
  waiting for transfers between devices  79.8 us (37%)
  starting transfers between devices  36.3 us (17%)
  blocking collectives  26.5 us (12%)
  local copies, waits for them, and re-layouts  25 us (12%)
  other arithmetic  22.5 us (10%)
  between operations  13.5 us (6%)
  matrix products  10.8 us (5%)
    all_to_all x1, waiting for transfers between devices, per_device(): lax.all_to_all(summed.astype(jnp.bfloat16), 'ka', split_axis=2, concat_ax...  28 us
    all_gather x1, blocking collectives, per_device(): lax.all_gather(trial_half, 'band', axis=2, tiled=True)  26.5 us
    all_to_all x1, waiting for transfers between devices, per_device(): lax.all_to_all(split_pairs, 'ka', split_axis=2, concat_axis=2, tiled=True)  25.5 us
    unnamed x2, other arithmetic  20.6 us
    all_to_all x2, starting transfers between devices, sent_to_all(): return lax.all_to_all(copies, axis, split_axis=0, concat_axis=0, tiled=True)  16.7 us
    gather x1, local copies, waits for them, and re-layouts, per_device(): jnp.take(lax.all_to_all(split_pairs, 'ka', split_axis=2, concat_axis=2, t...  13.9 us
    all_gather x1, waiting for transfers between devices, per_device(): lax.all_gather(vir_rows[0], 'band', axis=0, tiled=True)  13 us
    all_to_all x1, waiting for transfers between devices, summed_on_arrival(): pieces = lax.all_to_all(split_up(array, dim, size), axis, 0, 0, tiled=True)  12.6 us
  transfers between devices with their start and end apart: 6, of which 4 were waited for; matrix products, arithmetic and copies ran while one was open for 22% of the time, Pallas kernels for 0%

commit v1 on v0

v1 whole, which is shorter than its diff:
```python
import jax
import jax.numpy as jnp
from jax import lax
from jax.experimental import pallas as pl
from jax.experimental.pallas import tpu as pltpu
from jax.sharding import PartitionSpec as P

BF = jnp.bfloat16
F32 = jnp.float32
MESH = pl.DeviceIdType.MESH


def each(count, body):
    def step(i, carry):
        body(i)
        return carry

    lax.fori_loop(0, count, step, 0)


def rdma(src, dst, send, recv, ka, band):
    return pltpu.make_async_remote_copy(
        src_ref=src,
        dst_ref=dst,
        send_sem=send,
        recv_sem=recv,
        device_id={"ka": ka, "band": band},
        device_id_type=MESH,
    )


def kernel(
    minus, trial, occ, vir, coulomb, exch, out,
    trial_bf, trial_all, vir_x, occ_x, vir_t, t_all, occ_c, k_bf, k_f, pairs, s_bf, u_send, u_recv,
    dens1, dens2, coul, sig_send, sig_recv,
    tri_s, tri_r, x_s, x_r, o1_s, o1_r, o2_s, o2_r, o3_s, o3_r, t_s, t_r, d1_s, d1_r, d2_s, d2_r,
    u_s, u_r, g_s, g_r, loc,
):
    bands = lax.axis_size("band")
    chips = lax.axis_size("ka") // 2
    ka = lax.axis_index("ka")
    b = lax.axis_index("band")
    j = ka // 2
    c = lax.rem(ka, 2)
    o = 1 - c
    mine = 2 * j + c
    other = 2 * j + o
    rows, nocc = occ.shape
    width = trial.shape[1]
    nk = exch.shape[0]
    slab = rows // bands

    def band_peer(i):
        return lax.rem(b + 1 + i, bands)

    def chip_peer(i):
        return lax.rem(j + 1 + i, chips)

    load_k = pltpu.make_async_copy(
        exch.at[:, :, pl.ds(pl.multiple_of(j * rows, rows), rows)], k_bf, loc.at[0]
    )
    load_k.start()
    load_c = pltpu.make_async_copy(coulomb, coul, loc.at[1])
    load_c.start()

    barrier = pltpu.get_barrier_semaphore()

    def greet(k, band):
        pl.semaphore_signal(barrier, inc=1, device_id={"ka": k, "band": band}, device_id_type=MESH)

    def greet_band(i):
        greet(mine, band_peer(i))
        greet(other, band_peer(i))

    each(bands - 1, greet_band)
    greet(other, b)
    each(chips - 1, lambda i: greet(2 * chip_peer(i) + c, b))
    each(chips - 1, lambda i: greet(2 * chip_peer(i) + c, j))

    @pl.when(j != b)
    def _():
        greet(mine, j)

    trial_bf[...] = trial[...].astype(BF)
    callers = 2 * (bands - 1) + 1 + 2 * (chips - 1)
    pl.semaphore_wait(barrier, jnp.where(j == b, callers, callers + 1))

    own_cols = pl.ds(pl.multiple_of(b * width, 16), width)

    def tri_same(i):
        return rdma(trial_bf.at[c], trial_all.at[0, own_cols], tri_s.at[0, i], tri_r.at[0, b], mine, band_peer(i))

    def tri_cross(i):
        return rdma(trial_bf.at[o], trial_all.at[1, own_cols], tri_s.at[1, i], tri_r.at[1, b], other, lax.rem(b + i, bands))

    each(bands - 1, lambda i: tri_same(i).start())
    each(bands, lambda i: tri_cross(i).start())
    trial_all[0, own_cols, :] = trial_bf[c]

    def occ1(i):
        part = pl.ds(pl.multiple_of(i * slab, slab), slab)
        return rdma(occ.at[part], occ_c.at[c, j, part], o1_s.at[i], o1_r.at[j], 2 * b + c, i)

    def occ1_start(i):
        @pl.when((i != b) | (j != b))
        def _():
            occ1(i).start()

    each(bands, occ1_start)
    own_slab = pl.ds(pl.multiple_of(b * slab, slab), slab)

    @pl.when(j == b)
    def _():
        occ_c[c, j, own_slab, :] = occ[own_slab, :]

    send_vir = rdma(vir, vir_x, x_s.at[0], x_r.at[0], other, b)
    send_occ = rdma(occ, occ_x, x_s.at[1], x_r.at[1], other, b)
    send_vir.start()
    send_occ.start()

    def occ1_wait(i):
        @pl.when((i != j) | (j != b))
        def _():
            rdma(occ.at[own_slab], occ_c.at[c, i, own_slab], o1_s.at[i], o1_r.at[i], mine, i).wait_recv()

    each(chips, occ1_wait)

    def occ2(i):
        return rdma(
            occ_c.at[c, :, own_slab], occ_c.at[c, :, own_slab], o2_s.at[i], o2_r.at[b], mine, band_peer(i)
        )

    each(bands - 1, lambda i: occ2(i).start())

    send_vir.wait_recv()
    send_occ.wait_recv()
    vir_t[0] = vir[...].T
    vir_t[1] = vir_x[...].T

    def tri_wait(i):
        p = band_peer(i)
        cols = pl.ds(pl.multiple_of(p * width, 16), width)
        rdma(trial_bf.at[c], trial_all.at[0, cols], tri_s.at[0, i], tri_r.at[0, p], mine, p).wait_recv()

    def tri_wait_cross(i):
        cols = pl.ds(pl.multiple_of(i * width, 16), width)
        rdma(trial_bf.at[o], trial_all.at[1, cols], tri_s.at[1, i], tri_r.at[1, i], other, i).wait_recv()

    each(bands - 1, tri_wait)
    each(bands, tri_wait_cross)

    t_own = jnp.dot(vir[...], trial_all[0], preferred_element_type=F32)
    t_oth = jnp.dot(vir_x[...], trial_all[1], preferred_element_type=F32)
    t_all[mine] = t_own.astype(BF)
    t_all[other] = t_oth.astype(BF)
    pair_of = pl.ds(2 * j, 2)

    def t_copy(i):
        return rdma(t_all.at[pair_of], t_all.at[pair_of], t_s.at[i], t_r.at[j], 2 * chip_peer(i) + c, b)

    each(chips - 1, lambda i: t_copy(i).start())

    local = occ[...].astype(F32) * t_own + occ_x[...].astype(F32) * t_oth
    high = local.astype(BF)
    low = (local - high.astype(F32)).astype(BF)
    ones = jnp.ones((8, nocc), BF)
    along = (((1,), (1,)), ((), ()))
    dens1[j] = lax.dot_general(ones, high, along, preferred_element_type=F32) + lax.dot_general(
        ones, low, along, preferred_element_type=F32
    )

    def d1_copy(i):
        return rdma(dens1.at[j], dens1.at[j], d1_s.at[i], d1_r.at[j], 2 * chip_peer(i) + c, b)

    each(chips - 1, lambda i: d1_copy(i).start())

    load_k.wait()

    def widen(q):
        k_f[q] = k_bf[q].astype(F32)

    each(nk, widen)

    def occ2_wait(i):
        p = band_peer(i)
        part = pl.ds(pl.multiple_of(p * slab, slab), slab)
        rdma(occ_c.at[c, :, part], occ_c.at[c, :, part], o2_s.at[i], o2_r.at[p], mine, p).wait_recv()

    each(bands - 1, occ2_wait)
    occ3 = rdma(occ_c.at[c], occ_c.at[c], o3_s, o3_r, other, b)
    occ3.start()
    rdma(occ_c.at[c], occ_c.at[o], o3_s, o3_r, other, b).wait_recv()

    def pairs_of(p):
        for s in range(2):
            pairs[2 * p + s] = lax.dot_general(t_all[2 * p + s], occ_c[s, p], along, preferred_element_type=F32)

    pairs_of(j)

    def t_arrived(i):
        p = chip_peer(i)
        part = pl.ds(2 * p, 2)
        rdma(t_all.at[part], t_all.at[part], t_s.at[i], t_r.at[p], 2 * p + c, b).wait_recv()
        pairs_of(p)

    each(chips - 1, t_arrived)

    def d1_wait(i):
        p = chip_peer(i)
        rdma(dens1.at[p], dens1.at[p], d1_s.at[i], d1_r.at[p], 2 * p + c, b).wait_recv()

    each(chips - 1, d1_wait)
    total = dens1[0]
    for p in range(1, chips):
        total = total + dens1[p]
    dens2[b] = total

    def d2_copy(i):
        return rdma(dens2.at[b], dens2.at[b], d2_s.at[i], d2_r.at[b], mine, band_peer(i))

    each(bands - 1, lambda i: d2_copy(i).start())

    tile = 32
    fours = 4

    def screen(g):
        ks = []
        for n in range(fours):
            dest = j ^ (chips - 1 - 2 * g - n // 2)
            ks.append(2 * dest + n % 2)

        def rows_step(r):
            part = pl.ds(pl.multiple_of(r * tile, tile), tile)
            acc = [jnp.zeros((tile, rows), F32) for _ in ks]
            for q in range(nk):
                weight = k_f[q, part, :]
                for n, k in enumerate(ks):
                    acc[n] = acc[n] + pairs[minus[k, q], part, :] * weight
            for n in range(fours):
                s_bf[n, part, :] = acc[n].astype(BF)

        each(rows // tile, rows_step)
        for n, k in enumerate(ks):
            dest = k // 2
            u_send[k] = jnp.dot(s_bf[n], occ_c[n % 2, dest], preferred_element_type=F32).astype(BF)
            if n % 2 == 1:

                @pl.when(dest != j)
                def _():
                    u_copy(dest).start()

    def u_copy(dest):
        return rdma(u_send.at[pl.ds(2 * dest, 2)], u_recv.at[j], u_s.at[dest], u_r.at[j], 2 * dest + c, b)

    each(nk // fours, screen)

    def d2_wait(i):
        p = band_peer(i)
        rdma(dens2.at[p], dens2.at[p], d2_s.at[i], d2_r.at[p], mine, p).wait_recv()

    each(bands - 1, d2_wait)
    load_c.wait()
    pot = jnp.zeros((rows, nocc), F32)
    for p in range(bands):
        row = dens2[p][0:1, :].astype(BF)
        line = jnp.broadcast_to(row, (nocc, rows))
        pot = pot + lax.dot_general(coul[:, p * rows : (p + 1) * rows], line, along, preferred_element_type=F32)
    pot = pot * 2.0
    k_f[0, :, 0:nocc] = pot * occ[...].astype(F32) - u_send[mine].astype(F32)
    k_f[1, :, 0:nocc] = pot * occ_x[...].astype(F32) - u_send[other].astype(F32)

    def u_arrived(i):
        p = chip_peer(i)
        rdma(u_send.at[pl.ds(2 * p, 2)], u_recv.at[p], u_s.at[p], u_r.at[p], 2 * p + c, b).wait_recv()
        k_f[0, :, 0:nocc] = k_f[0, :, 0:nocc] - u_recv[p, c].astype(F32)
        k_f[1, :, 0:nocc] = k_f[1, :, 0:nocc] - u_recv[p, o].astype(F32)

    each(chips - 1, u_arrived)

    for s in range(2):
        sig_send[s] = jnp.dot(vir_t[s], k_f[s, :, 0:nocc].astype(BF), preferred_element_type=F32).astype(BF)

    def sig_same(i):
        p = band_peer(i)
        cols = pl.ds(pl.multiple_of(p * width, 16), width)
        return rdma(sig_send.at[0, cols], sig_recv.at[c, b], g_s.at[0, i], g_r.at[c, b], mine, p)

    def sig_cross(i):
        p = lax.rem(b + i, bands)
        cols = pl.ds(pl.multiple_of(p * width, 16), width)
        return rdma(sig_send.at[1, cols], sig_recv.at[c, b], g_s.at[1, i], g_r.at[c, b], other, p)

    each(bands - 1, lambda i: sig_same(i).start())
    each(bands, lambda i: sig_cross(i).start())
    sig_recv[c, b] = sig_send[0, own_cols, :]

    def sig_wait(i):
        p = band_peer(i)
        rdma(sig_send.at[0, own_cols], sig_recv.at[c, p], g_s.at[0, i], g_r.at[c, p], mine, p).wait_recv()

    def sig_wait_cross(i):
        rdma(sig_send.at[1, own_cols], sig_recv.at[o, i], g_s.at[1, i], g_r.at[o, i], other, i).wait_recv()

    each(bands - 1, sig_wait)
    each(bands, sig_wait_cross)
    for v in range(2):
        sums = sig_recv[v, 0].astype(F32)
        for p in range(1, bands):
            sums = sums + sig_recv[v, p].astype(F32)
        out[v] = sums

    each(bands - 1, lambda i: tri_same(i).wait_send())
    each(bands, lambda i: tri_cross(i).wait_send())

    def occ1_sent(i):
        @pl.when((i != b) | (j != b))
        def _():
            occ1(i).wait_send()

    each(bands, occ1_sent)
    send_vir.wait_send()
    send_occ.wait_send()
    each(bands - 1, lambda i: occ2(i).wait_send())
    occ3.wait_send()
    each(chips - 1, lambda i: t_copy(i).wait_send())
    each(chips - 1, lambda i: d1_copy(i).wait_send())
    each(bands - 1, lambda i: d2_copy(i).wait_send())
    each(chips - 1, lambda i: u_copy(chip_peer(i)).wait_send())
    each(bands - 1, lambda i: sig_same(i).wait_send())
    each(bands, lambda i: sig_cross(i).wait_send())


def solution(mesh):
    bands = mesh.shape["band"]
    chips = mesh.shape["ka"] // 2

    def per_device(occ, vir, trial, occ_energy, vir_energy, coulomb, exch, minus):
        nk, rows, aux = exch.shape
        nocc = occ.shape[2]
        nvir = vir.shape[2]
        width = trial.shape[3]
        turned = jnp.transpose(trial[0], (0, 2, 1))
        vmem = pl.BlockSpec(memory_space=pltpu.VMEM)
        far = pl.BlockSpec(memory_space=pl.ANY)
        dma = pltpu.SemaphoreType.DMA
        coupled = pl.pallas_call(
            kernel,
            out_shape=jax.ShapeDtypeStruct((2, width, nocc), F32),
            in_specs=[pl.BlockSpec(memory_space=pltpu.SMEM), vmem, vmem, vmem, far, far],
            out_specs=vmem,
            scratch_shapes=[
                pltpu.VMEM((2, width, nocc), BF),
                pltpu.VMEM((2, nvir, nocc), BF),
                pltpu.VMEM((rows, nvir), BF),
                pltpu.VMEM((rows, nocc), BF),
                pltpu.VMEM((2, nvir, rows), BF),
                pltpu.VMEM((nk, rows, nocc), BF),
                pltpu.VMEM((2, chips, rows, nocc), BF),
                pltpu.VMEM((nk, rows, rows), BF),
                pltpu.VMEM((nk, rows, rows), F32),
                pltpu.VMEM((nk, rows, rows), F32),
                pltpu.VMEM((4, rows, rows), BF),
                pltpu.VMEM((nk, rows, nocc), BF),
                pltpu.VMEM((chips, 2, rows, nocc), BF),
                pltpu.VMEM((chips, 8, rows), F32),
                pltpu.VMEM((bands, 8, rows), F32),
                pltpu.VMEM((rows, aux), BF),
                pltpu.VMEM((2, nvir, nocc), BF),
                pltpu.VMEM((2, bands, width, nocc), BF),
                dma((2, bands)), dma((2, bands)),
                dma((2,)), dma((2,)),
                dma((bands,)), dma((chips,)),
                dma((bands,)), dma((bands,)),
                dma, dma,
                dma((chips,)), dma((chips,)),
                dma((chips,)), dma((chips,)),
                dma((bands,)), dma((bands,)),
                dma((chips,)), dma((chips,)),
                dma((2, bands)), dma((2, bands)),
                dma((2,)),
            ],
            compiler_params=pltpu.CompilerParams(
                collective_id=0, has_side_effects=True, vmem_limit_bytes=48 * 1024 * 1024
            ),
            name="sigma",
        )(minus, turned, occ[0], vir[0], coulomb, exch)
        gaps = vir_energy[0][None, :] - occ_energy[0][:, None]
        return (gaps[None] * trial[0] + jnp.transpose(coupled, (0, 2, 1)))[None]

    in_specs = (
        P("ka", "band", None),
        P("ka", "band", None),
        P("ka", None, None, "band"),
        P("ka", None),
        P("ka", "band"),
        P("band", None),
        P(None, "band", None),
        P(),
    )
    return jax.shard_map(
        per_device,
        mesh=mesh,
        in_specs=in_specs,
        out_specs=P("ka", None, None, "band"),
        check_vma=False,
    )
```

time: 216 us -> 72.5 us (0.34)
  waiting for transfers between devices: 79.8 us -> 0 us
  Pallas kernels: 0 us -> 66.1 us
  starting transfers between devices: 36.3 us -> 0 us
  blocking collectives: 26.5 us -> 0 us
  other arithmetic: 22.5 us -> 1.41 us
  local copies, waits for them, and re-layouts: 25 us -> 4.67 us
  between operations: 13.5 us -> 0.03 us
  matrix products: 10.8 us -> 0 us
    pallas_call x0 -> x1, Pallas kernels: none -> 66.1 us  [per_device(): pl.pallas_call(kernel, out_shape=jax.ShapeDtypeStruct((2, width, nocc), F...]
    all_to_all x5 -> x0, waiting for transfers between devices: 66 us -> none  [the longest x1 28 us: per_device(): lax.all_to_all(summed.astype(jnp.bfloat16), 'ka', split_axis=2, concat_ax...]
    all_to_all x5 -> x0, starting transfers between devices: 36.3 us -> none  [the longest x2 16.7 us: sent_to_all(): return lax.all_to_all(copies, axis, split_axis=0, concat_axis=0, tiled=True)]
    all_gather x1 -> x0, blocking collectives: 26.5 us -> none  [per_device(): lax.all_gather(trial_half, 'band', axis=2, tiled=True)]
    unnamed x2 -> x0, other arithmetic: 20.6 us -> none
    gather x1 -> x0, local copies, waits for them, and re-layouts: 13.9 us -> none  [per_device(): jnp.take(lax.all_to_all(split_pairs, 'ka', split_axis=2, concat_axis=2, t...]
    all_gather x1 -> x0, waiting for transfers between devices: 13 us -> none  [per_device(): lax.all_gather(vir_rows[0], 'band', axis=0, tiled=True)]
    dot_general x4 -> x0, matrix products: 10.8 us -> none  [the longest x1 5.56 us: per_device(): jnp.einsum('ri,vra->via', occ_own, weights, preferred_element_type=jnp.fl...]
  transfers between devices with their start and end apart: 6 -> 0, of which waited for: 4 -> 0; matrix products, arithmetic and copies ran while one was open for 22% -> 0% of each run, Pallas kernels for 0% -> 0%
where the time goes in v1:
time: 72.5 us; the launch traced here: 72.2 us
  Pallas kernels  66.1 us (91%)
  local copies, waits for them, and re-layouts  4.67 us (6%)
  other arithmetic  1.41 us (2%)
    pallas_call x1, Pallas kernels, per_device(): pl.pallas_call(kernel, out_shape=jax.ShapeDtypeStruct((2, width, nocc), F...  66.1 us
    unnamed x10, local copies, waits for them, and re-layouts  4.67 us

profile of v1, /device:TPU:1, one launch (start us, length us, event | category | flops | bytes accessed | tf_op | source)
XLA Modules:
  0.0 72.2 jit_solution(61842137832830855)
XLA Ops:
  0.0 0.7 %broadcast_subtract_fusion = f32[128,112]{0,1:T(8,128)S(1)} fusion(f32[128]{0:T(128)} %bitcast.19, f32[112]{0:T(128)} %bitcast.20), kind=kLoop, calls=%fused_computation.3 | loop fusion | flops 14336 | bytes 58304 | tf_op jit(solution)/shard_map/sub | solution.py:387
  0.8 0.0 copy-start
  0.8 1.2 %copy-done = bf16[256,2048]{1,0:T(8,128)(2,1)S(1)} copy-done((bf16[256,2048]{1,0:T(8,128)(2,1)S(1)}, bf16[256,2048]{1,0:T(8,128)(2,1)}, u32[]{:S(2)}) %copy-start) | copy-done | bytes 1048600
  2.0 0.0 copy-start.1
  2.0 1.0 %copy-done.1 = bf16[1,256,896]{2,1,0:T(8,128)(2,1)S(1)} copy-done((bf16[1,256,896]{2,1,0:T(8,128)(2,1)S(1)}, bf16[1,256,896]{2,1,0:T(8,128)(2,1)}, u32[]{:S(2)}) %copy-start.1) | copy-done | bytes 458776
  3.0 0.0 copy-start.2
  3.0 0.9 %copy-done.2 = f32[1,2,128,112]{2,3,1,0:T(8,128)S(1)} copy-done((f32[1,2,128,112]{2,3,1,0:T(8,128)S(1)}, f32[1,2,128,112]{2,3,1,0:T(8,128)}, u32[]{:S(2)}) %copy-start.2) | copy-done | bytes 114712
  3.9 0.0 copy-start.3
  3.9 0.8 %copy-done.3 = bf16[1,256,128]{2,1,0:T(8,128)(2,1)S(1)} copy-done((bf16[1,256,128]{2,1,0:T(8,128)(2,1)S(1)}, bf16[1,256,128]{2,1,0:T(8,128)(2,1)}, u32[]{:S(2)}) %copy-start.3) | copy-done | bytes 65560
  4.7 0.0 copy-start.4
  4.7 0.7 copy-done.4
  5.4 66.1 %sigma.1 = f32[2,112,128]{2,1,0:T(8,128)S(1)} custom-call(s32[16,16]{1,0:T(8,128)S(1)} %copy-done.4, f32[2,112,128]{2,1,0:T(8,128)S(1)} %bitcast.17, bf16[256,128]{1,0:T(8,128)(2,1)S(1)} %bitcast.18, bf16[256,896]{1,0:T(8,128)(2,1)S(1)} %bitcast.16, bf16[256,2048]{1,0:T(8,128)(2,1)S(1)} %copy-done, bf16[16,256,2048]{2,1,0:T(8,128)(2,1)} %exch.1), custom_call_target="tpu_custom_call" | custom-call | tf_op jit(solution)/shard_map/sigma/pallas_call | solution.py:346
  71.6 0.7 fusion
Async XLA Ops:
  0.8 1.2 %copy-start = (bf16[256,2048]{1,0:T(8,128)(2,1)S(1)}, bf16[256,2048]{1,0:T(8,128)(2,1)}, u32[]{:S(2)}) copy-start(bf16[256,2048]{1,0:T(8,128)(2,1)} %coulomb.1) | copy-start | bytes 3145732
  2.0 1.0 %copy-start.1 = (bf16[1,256,896]{2,1,0:T(8,128)(2,1)S(1)}, bf16[1,256,896]{2,1,0:T(8,128)(2,1)}, u32[]{:S(2)}) copy-start(bf16[1,256,896]{2,1,0:T(8,128)(2,1)} %param.9) | copy-start | bytes 1376260
  3.0 0.9 %copy-start.2 = (f32[1,2,128,112]{2,3,1,0:T(8,128)S(1)}, f32[1,2,128,112]{2,3,1,0:T(8,128)}, u32[]{:S(2)}) copy-start(f32[1,2,128,112]{2,3,1,0:T(8,128)} %param.10) | copy-start | bytes 344068
  3.9 0.8 %copy-start.3 = (bf16[1,256,128]{2,1,0:T(8,128)(2,1)S(1)}, bf16[1,256,128]{2,1,0:T(8,128)(2,1)}, u32[]{:S(2)}) copy-start(bf16[1,256,128]{2,1,0:T(8,128)(2,1)} %param.8) | copy-start | bytes 196612
  4.7 0.7 copy-start.4

commit v2 on v1

v2 whole, which is shorter than its diff:
```python
import jax
import jax.numpy as jnp
from jax import lax
from jax.experimental import pallas as pl
from jax.experimental.pallas import tpu as pltpu
from jax.sharding import PartitionSpec as P

BF = jnp.bfloat16
F32 = jnp.float32
MESH = pl.DeviceIdType.MESH
ALONG = (((1,), (1,)), ((), ()))


def each(count, body):
    def step(i, carry):
        body(i)
        return carry

    lax.fori_loop(0, count, step, 0)


def rdma(src, dst, send, recv, ka, band):
    return pltpu.make_async_remote_copy(
        src_ref=src,
        dst_ref=dst,
        send_sem=send,
        recv_sem=recv,
        device_id={"ka": ka, "band": band},
        device_id_type=MESH,
    )


def kernel(
    minus_h, trial_h, occ_h, vir_h, coulomb, exch, out,
    minus, trial, occ, vir, trial_bf, trial_all, vir_t, t_mine, t_all, occ_c, k_bf, k_f, pairs, s_bf,
    u_send, u_recv, acc_w, dens1, dens2, coul, sig_send, sig_recv,
    tri_s, tri_r, x_s, x_r, o1_s, o1_r, ox_s, ox_r, oy_s, oy_r, o3_s, o3_r, t_s, t_r, d1_s, d1_r, d2_s, d2_r,
    u_s, u_r, g_s, g_r, loc,
):
    bands = lax.axis_size("band")
    chips = lax.axis_size("ka") // 2
    depth = chips // 2
    ka = lax.axis_index("ka")
    b = lax.axis_index("band")
    j = ka // 2
    c = lax.rem(ka, 2)
    o = 1 - c
    h = j // depth
    z = lax.rem(j, depth)
    side = bands // 2
    xl = b // side
    y = lax.rem(b, side)
    quarter = 2 * h + xl
    mine = 2 * j + c
    other = 2 * j + o
    rows, nocc = occ_h.shape
    half = rows // 2
    width = trial.shape[1]
    nk = exch.shape[0]
    slab = rows // bands
    cols = pairs.shape[2]
    home = 2 * z + h
    goal = lax.rem(b, 2) * depth + b // 2

    def band_peer(i):
        return lax.rem(b + 1 + i, bands)

    def chip_peer(i):
        return lax.rem(j + 1 + i, chips)

    def block(start, size, unit=16):
        return pl.ds(pl.multiple_of(start, unit), size)

    loads = [
        pltpu.make_async_copy(occ_h, occ.at[c], loc.at[0]),
        pltpu.make_async_copy(trial_h, trial, loc.at[1]),
        pltpu.make_async_copy(vir_h, vir.at[c], loc.at[2]),
        pltpu.make_async_copy(
            exch.at[:, block(h * half, half), block(z * cols, cols, 128)], k_bf, loc.at[3]
        ),
        pltpu.make_async_copy(minus_h, minus, loc.at[4]),
        pltpu.make_async_copy(coulomb, coul, loc.at[5]),
    ]
    for load in loads:
        load.start()

    barrier = pltpu.get_barrier_semaphore()

    def greet(k, band):
        pl.semaphore_signal(barrier, inc=1, device_id={"ka": k, "band": band}, device_id_type=MESH)

    def greet_band(i):
        greet(mine, band_peer(i))
        greet(other, band_peer(i))

    def greet_chip(i):
        greet(2 * chip_peer(i) + c, b)
        greet(2 * chip_peer(i) + c, home)

    each(bands - 1, greet_band)
    each(chips - 1, greet_chip)
    greet(other, b)
    greet(2 * ((1 - h) * depth + z) + c, (1 - xl) * side + y)

    @pl.when(home != b)
    def _():
        greet(mine, home)

    loads[0].wait()
    loads[1].wait()
    trial_bf[...] = trial[...].astype(BF)
    callers = 2 * (bands - 1) + 2 * (chips - 1) + 2
    pl.semaphore_wait(barrier, jnp.where(home == b, callers, callers + 1))

    def occ1(i):
        return rdma(
            occ.at[c, block(i * slab, slab)],
            occ_c.at[c, j, 2 * lax.rem(b, 2) + i // side, lax.rem(i, side)],
            o1_s.at[i], o1_r.at[j], 2 * goal + c, i,
        )

    def occ1_start(i):
        @pl.when((i != b) | (goal != j))
        def _():
            occ1(i).start()

    each(bands, occ1_start)

    @pl.when(home == b)
    def _():
        occ_c[c, j, quarter, y] = occ[c, block(b * slab, slab), :]

    own_cols = block(b * width, width)

    def tri_same(i):
        return rdma(trial_bf.at[c], trial_all.at[c, own_cols], tri_s.at[0, i], tri_r.at[c, b], mine, band_peer(i))

    def tri_cross(i):
        p = lax.rem(b + i, bands)
        return rdma(trial_bf.at[o], trial_all.at[c, own_cols], tri_s.at[1, i], tri_r.at[c, b], other, p)

    each(bands - 1, lambda i: tri_same(i).start())
    loads[2].wait()
    send_vir = rdma(vir.at[c], vir.at[c], x_s.at[0], x_r.at[0], other, b)
    send_occ = rdma(occ.at[c], occ.at[c], x_s.at[1], x_r.at[1], other, b)
    send_vir.start()
    send_occ.start()
    each(bands, lambda i: tri_cross(i).start())
    trial_all[c, own_cols, :] = trial_bf[c]

    def occ1_wait(i):
        @pl.when((i != j) | (home != b))
        def _():
            rdma(
                occ.at[c, block(b * slab, slab)], occ_c.at[c, i, quarter, y], o1_s.at[i], o1_r.at[i], mine, b
            ).wait_recv()

    each(chips, occ1_wait)

    def piece(q, row):
        return occ_c.at[c, :, q, row]

    def occ_x(i):
        q = quarter ^ (i + 1)
        return rdma(
            piece(quarter, y), piece(quarter, y), ox_s.at[i], ox_r.at[quarter],
            2 * ((q // 2) * depth + z) + c, lax.rem(q, 2) * side + y,
        )

    def occ_y(q, i):
        return rdma(
            piece(q, y), piece(q, y), oy_s.at[q, i], oy_r.at[q, y], mine, xl * side + lax.rem(y + 1 + i, side)
        )

    each(3, lambda i: occ_x(i).start())
    each(side - 1, lambda i: occ_y(quarter, i).start())

    vir_t[c] = vir[c].T

    def tri_wait_same(i):
        p = band_peer(i)
        part = block(p * width, width)
        rdma(trial_bf.at[c], trial_all.at[c, part], tri_s.at[0, i], tri_r.at[c, p], mine, p).wait_recv()

    def tri_wait_cross(i):
        part = block(i * width, width)
        rdma(trial_bf.at[o], trial_all.at[o, part], tri_s.at[1, i], tri_r.at[o, i], other, i).wait_recv()

    def t_copy(s, i):
        p = chip_peer(i)
        return rdma(t_mine.at[p // depth, s], t_all.at[2 * j + s], t_s.at[s, i], t_r.at[s, j], 2 * p + c, b)

    def t_make(s):
        value = jnp.dot(vir[s], trial_all[s], preferred_element_type=F32)
        t_mine[0, s] = value[:half].astype(BF)
        t_mine[1, s] = value[half:].astype(BF)
        each(chips - 1, lambda i: t_copy(s, i).start())
        t_all[2 * j + s] = t_mine[h, s]
        return occ[s].astype(F32) * value

    each(bands - 1, tri_wait_same)
    local = t_make(c)
    rdma(vir.at[c], vir.at[o], x_s.at[0], x_r.at[0], other, b).wait_recv()
    rdma(occ.at[c], occ.at[o], x_s.at[1], x_r.at[1], other, b).wait_recv()
    each(bands, tri_wait_cross)
    local = local + t_make(o)

    def forward(i):
        q = quarter ^ (i + 1)
        rdma(piece(quarter, y), piece(q, y), ox_s.at[i], ox_r.at[q], mine, b).wait_recv()
        each(side - 1, lambda n: occ_y(q, n).start())

    each(3, forward)

    def occ3(row):
        return rdma(occ_c.at[c, :, :, row], occ_c.at[c, :, :, row], o3_s.at[row], o3_r.at[row], other, b)

    occ3(y).start()

    high = local.astype(BF)
    low = (local - high.astype(F32)).astype(BF)
    ones = jnp.ones((8, nocc), BF)
    dens1[j] = lax.dot_general(ones, high, ALONG, preferred_element_type=F32) + lax.dot_general(
        ones, low, ALONG, preferred_element_type=F32
    )

    def d1_copy(i):
        return rdma(dens1.at[j], dens1.at[j], d1_s.at[i], d1_r.at[j], 2 * chip_peer(i) + c, b)

    each(chips - 1, lambda i: d1_copy(i).start())
    vir_t[o] = vir[o].T

    loads[3].wait()

    def widen(q):
        k_f[q] = k_bf[q].astype(F32)

    each(nk, widen)

    def occ_rest(i):
        row = lax.rem(y + 1 + i, side)
        for q in range(4):
            rdma(piece(q, row), piece(q, row), oy_s.at[q, i], oy_r.at[q, row], mine, b).wait_recv()
        occ3(row).start()

    each(side - 1, occ_rest)

    def occ3_wait(row):
        rdma(occ_c.at[c, :, :, row], occ_c.at[o, :, :, row], o3_s.at[row], o3_r.at[row], other, b).wait_recv()

    each(side, occ3_wait)

    def pairs_of(p):
        for s in range(2):
            points = occ_c[s, p].reshape(cols, nocc)
            pairs[2 * p + s] = lax.dot_general(t_all[2 * p + s], points, ALONG, preferred_element_type=F32)

    pairs_of(j)

    def t_arrived(i):
        p = chip_peer(i)
        for s in range(2):
            rdma(t_mine.at[0, s], t_all.at[2 * p + s], t_s.at[s, i], t_r.at[s, p], 2 * p + c, b).wait_recv()
        pairs_of(p)

    each(chips - 1, t_arrived)

    def d1_wait(i):
        p = chip_peer(i)
        rdma(dens1.at[p], dens1.at[p], d1_s.at[i], d1_r.at[p], 2 * p + c, b).wait_recv()

    each(chips - 1, d1_wait)
    total = dens1[0]
    for p in range(1, chips):
        total = total + dens1[p]
    dens2[b] = total

    def d2_copy(i):
        return rdma(dens2.at[b], dens2.at[b], d2_s.at[i], d2_r.at[b], mine, band_peer(i))

    each(bands - 1, lambda i: d2_copy(i).start())
    loads[4].wait()

    tile = 16
    fours = 4

    def u_copy(dest, s):
        return rdma(u_send.at[2 * dest + s], u_recv.at[j, s], u_s.at[s, dest], u_r.at[s, j], 2 * dest + c, b)

    def screen(g, s):
        dests = [j ^ (chips - 1 - fours * g - n) for n in range(fours)]

        def rows_step(r):
            part = block(r * tile, tile)
            acc = [jnp.zeros((tile, cols), F32) for _ in dests]
            for q in range(nk):
                weight = k_f[q, part, :]
                for n, dest in enumerate(dests):
                    acc[n] = acc[n] + pairs[minus[2 * dest + s, q], part, :] * weight
            for n in range(fours):
                s_bf[n, part, :] = acc[n].astype(BF)

        each(half // tile, rows_step)
        for n, dest in enumerate(dests):
            points = occ_c[s, dest].reshape(cols, nocc)
            u_send[2 * dest + s] = jnp.dot(s_bf[n], points, preferred_element_type=F32).astype(BF)

            @pl.when(dest != j)
            def _():
                u_copy(dest, s).start()

    def finish(s):
        mine_rows = block(h * half, half)
        acc_w[s, mine_rows, :] = acc_w[s, mine_rows, :] - u_send[2 * j + s].astype(F32)

        def u_arrived(i):
            p = chip_peer(i)
            rdma(u_send.at[2 * p + s], u_recv.at[p, s], u_s.at[s, p], u_r.at[s, p], 2 * p + c, b).wait_recv()
            part = block((p // depth) * half, half)
            acc_w[s, part, :] = acc_w[s, part, :] - u_recv[p, s].astype(F32)

        each(chips - 1, u_arrived)
        sig_send[s] = jnp.dot(vir_t[s], acc_w[s].astype(BF), preferred_element_type=F32).astype(BF)

        def sig_start(p):
            @pl.when((c != s) | (p != b))
            def _():
                sig_copy(s, p).start()

        each(bands, sig_start)

        @pl.when(c == s)
        def _():
            sig_recv[c, b] = sig_send[s, own_cols, :]

    def sig_copy(s, p):
        return rdma(
            sig_send.at[s, block(p * width, width)], sig_recv.at[c, b], g_s.at[s, p], g_r.at[c, b], 2 * j + s, p
        )

    screen(0, 0)
    screen(1, 0)
    screen(0, 1)

    def d2_wait(i):
        p = band_peer(i)
        rdma(dens2.at[p], dens2.at[p], d2_s.at[i], d2_r.at[p], mine, p).wait_recv()

    each(bands - 1, d2_wait)
    loads[5].wait()
    pot = jnp.zeros((rows, nocc), F32)
    for p in range(bands):
        line = jnp.broadcast_to(dens2[p][0:1, :].astype(BF), (nocc, rows))
        pot = pot + lax.dot_general(coul[:, p * rows : (p + 1) * rows], line, ALONG, preferred_element_type=F32)
    pot = pot * 2.0
    for s in range(2):
        acc_w[s] = pot * occ[s].astype(F32)

    finish(0)
    screen(1, 1)
    finish(1)

    def sig_wait_same(i):
        p = band_peer(i)
        rdma(sig_send.at[0, own_cols], sig_recv.at[c, p], g_s.at[0, i], g_r.at[c, p], mine, p).wait_recv()

    def sig_wait_cross(i):
        rdma(sig_send.at[0, own_cols], sig_recv.at[o, i], g_s.at[1, i], g_r.at[o, i], other, i).wait_recv()

    each(bands - 1, sig_wait_same)
    each(bands, sig_wait_cross)
    for v in range(2):
        sums = sig_recv[v, 0].astype(F32)
        for p in range(1, bands):
            sums = sums + sig_recv[v, p].astype(F32)
        out[v] = sums

    each(bands - 1, lambda i: tri_same(i).wait_send())
    each(bands, lambda i: tri_cross(i).wait_send())

    def occ1_sent(i):
        @pl.when((i != b) | (goal != j))
        def _():
            occ1(i).wait_send()

    each(bands, occ1_sent)
    send_vir.wait_send()
    send_occ.wait_send()
    each(3, lambda i: occ_x(i).wait_send())
    for q in range(4):
        each(side - 1, lambda i: occ_y(q, i).wait_send())
    each(side, lambda row: occ3(row).wait_send())
    each(chips - 1, lambda i: d1_copy(i).wait_send())
    each(bands - 1, lambda i: d2_copy(i).wait_send())
    for s in range(2):
        each(chips - 1, lambda i: t_copy(s, i).wait_send())
        each(chips - 1, lambda i: u_copy(chip_peer(i), s).wait_send())

        def sig_sent(p):
            @pl.when((c != s) | (p != b))
            def _():
                sig_copy(s, p).wait_send()

        each(bands, sig_sent)


def solution(mesh):
    bands = mesh.shape["band"]
    chips = mesh.shape["ka"] // 2

    def per_device(occ, vir, trial, occ_energy, vir_energy, coulomb, exch, minus):
        nk, rows, aux = exch.shape
        nocc = occ.shape[2]
        nvir = vir.shape[2]
        width = trial.shape[3]
        half = rows // 2
        cols = 2 * rows
        turned = jnp.transpose(trial[0], (0, 2, 1))
        far = pl.BlockSpec(memory_space=pltpu.HBM)
        dma = pltpu.SemaphoreType.DMA
        coupled = pl.pallas_call(
            kernel,
            out_shape=jax.ShapeDtypeStruct((2, width, nocc), F32),
            in_specs=[far] * 6,
            out_specs=pl.BlockSpec(memory_space=pltpu.VMEM),
            scratch_shapes=[
                pltpu.SMEM((nk, nk), jnp.int32),
                pltpu.VMEM((2, width, nocc), F32),
                pltpu.VMEM((2, rows, nocc), BF),
                pltpu.VMEM((2, rows, nvir), BF),
                pltpu.VMEM((2, width, nocc), BF),
                pltpu.VMEM((2, nvir, nocc), BF),
                pltpu.VMEM((2, nvir, rows), BF),
                pltpu.VMEM((2, 2, half, nocc), BF),
                pltpu.VMEM((nk, half, nocc), BF),
                pltpu.VMEM((2, chips, 4, bands // 2, rows // bands, nocc), BF),
                pltpu.VMEM((nk, half, cols), BF),
                pltpu.VMEM((nk, half, cols), F32),
                pltpu.VMEM((nk, half, cols), F32),
                pltpu.VMEM((4, half, cols), BF),
                pltpu.VMEM((nk, half, nocc), BF),
                pltpu.VMEM((chips, 2, half, nocc), BF),
                pltpu.VMEM((2, rows, nocc), F32),
                pltpu.VMEM((chips, 8, rows), F32),
                pltpu.VMEM((bands, 8, rows), F32),
                pltpu.VMEM((rows, aux), BF),
                pltpu.VMEM((2, nvir, nocc), BF),
                pltpu.VMEM((2, bands, width, nocc), BF),
                dma((2, bands)), dma((2, bands)),
                dma((2,)), dma((2,)),
                dma((bands,)), dma((chips,)),
                dma((3,)), dma((4,)),
                dma((4, bands // 2)), dma((4, bands // 2)),
                dma((bands // 2,)), dma((bands // 2,)),
                dma((2, chips)), dma((2, chips)),
                dma((chips,)), dma((chips,)),
                dma((bands,)), dma((bands,)),
                dma((2, chips)), dma((2, chips)),
                dma((2, bands)), dma((2, bands)),
                dma((6,)),
            ],
            compiler_params=pltpu.CompilerParams(
                collective_id=0, has_side_effects=True, vmem_limit_bytes=67043328
            ),
            name="sigma",
        )(minus, turned, occ[0], vir[0], coulomb, exch)
        gaps = vir_energy[0][None, :] - occ_energy[0][:, None]
        return (gaps[None] * trial[0] + jnp.transpose(coupled, (0, 2, 1)))[None]

    in_specs = (
        P("ka", "band", None),
        P("ka", "band", None),
        P("ka", None, None, "band"),
        P("ka", None),
        P("ka", "band"),
        P("band", None),
        P(None, "band", None),
        P(),
    )
    return jax.shard_map(
        per_device,
        mesh=mesh,
        in_specs=in_specs,
        out_specs=P("ka", None, None, "band"),
        check_vma=False,
    )
```

time: 72.5 us -> 60.1 us (0.83)
  Pallas kernels: 66.1 us -> 56.9 us
  local copies, waits for them, and re-layouts: 4.67 us -> 0 us
  other arithmetic: 1.41 us -> 3 us
    pallas_call x1, Pallas kernels: 66.1 us -> 56.9 us  [per_device(): pl.pallas_call(kernel, out_shape=jax.ShapeDtypeStruct((2, width, nocc), F...]
    unnamed x10 -> x0, local copies, waits for them, and re-layouts: 4.67 us -> none
    broadcast_in_dim x1, other arithmetic: 0.66 us -> 1.62 us  [per_device(): return (gaps[None] * trial[0] + jnp.transpose(coupled, (0, 2, 1)))[None]]
where the time goes in v2:
time: 60.1 us; the launch traced here: 59.9 us
  Pallas kernels  56.9 us (95%)
  other arithmetic  3 us (5%)
    pallas_call x1, Pallas kernels, per_device(): pl.pallas_call(kernel, out_shape=jax.ShapeDtypeStruct((2, width, nocc), F...  56.9 us
    broadcast_in_dim x1, other arithmetic, per_device(): return (gaps[None] * trial[0] + jnp.transpose(coupled, (0, 2, 1)))[None]  1.62 us
    sub x1, other arithmetic, per_device(): gaps = vir_energy[0][None, :] - occ_energy[0][:, None]  1.38 us

profile of v2, /device:TPU:1, one launch (start us, length us, event | category | flops | bytes accessed | tf_op | source)
XLA Modules:
  0.0 59.9 jit_solution(10004684742545276542)
XLA Ops:
  0.0 1.4 %broadcast_subtract_fusion = f32[128,112]{0,1:T(8,128)} fusion(f32[128]{0:T(128)} %bitcast.19, f32[112]{0:T(128)} %bitcast.20), kind=kLoop, calls=%fused_computation.3 | loop fusion | flops 14336 | bytes 58304 | tf_op jit(solution)/shard_map/sub | solution.py:467
  1.4 56.9 %sigma.1 = f32[2,112,128]{2,1,0:T(8,128)} custom-call(s32[16,16]{1,0:T(8,128)} %minus_h.1, f32[2,112,128]{2,1,0:T(8,128)} %bitcast.17, bf16[256,128]{1,0:T(8,128)(2,1)} %bitcast.18, bf16[256,896]{1,0:T(8,128)(2,1)} %bitcast.16, bf16[256,2048]{1,0:T(8,128)(2,1)} %coulomb.1, bf16[16,256,2048]{2,1,0:T(8,128)(2,1)} %exch.1), custom_call_target="tpu_custom_call" | custom-call | tf_op jit(solution)/shard_map/sigma/pallas_call | solution.py:421
  58.3 1.6 %fusion = f32[1,2,128,112]{2,3,1,0:T(8,128)} fusion(f32[2,112,128]{2,1,0:T(8,128)} %sigma.1, f32[1,2,128,112]{2,3,1,0:T(8,128)} %param.10, f32[128,112]{0,1:T(8,128)} %broadcast_subtract_fusion), kind=kLoop, calls=%fused_computation.1 | loop fusion | flops 57344 | bytes 401408 | tf_op jit(solution)/shard_map/broadcast_in_dim | solution.py:468

commit v3 on v2

--- a/solution.py
+++ b/solution.py
@@ -31,8 +31,8 @@
 
 
 def kernel(
-    minus_h, trial_h, occ_h, vir_h, coulomb, exch, out,
-    minus, trial, occ, vir, trial_bf, trial_all, vir_t, t_mine, t_all, occ_c, k_bf, k_f, pairs, s_bf,
+    minus_h, trial_h, occ_h, vir_h, coulomb, exch, occ_e_h, vir_e_h, out,
+    minus, trial, occ, vir, occ_e, vir_e, turn, trial_bf, trial_all, vir_t, t_mine, t_all, occ_c, k_bf, pairs, s_bf,
     u_send, u_recv, acc_w, dens1, dens2, coul, sig_send, sig_recv,
     tri_s, tri_r, x_s, x_r, o1_s, o1_r, ox_s, ox_r, oy_s, oy_r, o3_s, o3_r, t_s, t_r, d1_s, d1_r, d2_s, d2_r,
     u_s, u_r, g_s, g_r, loc,
@@ -80,6 +80,8 @@
         ),
         pltpu.make_async_copy(minus_h, minus, loc.at[4]),
         pltpu.make_async_copy(coulomb, coul, loc.at[5]),
+        pltpu.make_async_copy(occ_e_h, occ_e, loc.at[6]),
+        pltpu.make_async_copy(vir_e_h, vir_e, loc.at[7]),
     ]
     for load in loads:
         load.start()
@@ -167,13 +169,22 @@
             2 * ((q // 2) * depth + z) + c, lax.rem(q, 2) * side + y,
         )
 
-    def occ_y(q, i):
-        return rdma(
-            piece(q, y), piece(q, y), oy_s.at[q, i], oy_r.at[q, y], mine, xl * side + lax.rem(y + 1 + i, side)
-        )
+    up = lax.rem(y + 1, side)
+    down = lax.rem(y + side - 1, side)
+    across = lax.rem(y + 2, side)
+
+    def occ_y(q, row, to, n):
+        return rdma(piece(q, row), piece(q, row), oy_s.at[q, n], oy_r.at[q, row], mine, xl * side + to)
+
+    def occ_y_start(q):
+        occ_y(q, y, up, 0).start()
+        occ_y(q, y, down, 1).start()
+
+    def occ_y_wait(q, row):
+        rdma(piece(q, row), piece(q, row), oy_s.at[q, 0], oy_r.at[q, row], mine, b).wait_recv()
 
     each(3, lambda i: occ_x(i).start())
-    each(side - 1, lambda i: occ_y(quarter, i).start())
+    occ_y_start(quarter)
 
     vir_t[c] = vir[c].T
 
@@ -194,28 +205,19 @@
         value = jnp.dot(vir[s], trial_all[s], preferred_element_type=F32)
         t_mine[0, s] = value[:half].astype(BF)
         t_mine[1, s] = value[half:].astype(BF)
-        each(chips - 1, lambda i: t_copy(s, i).start())
         t_all[2 * j + s] = t_mine[h, s]
         return occ[s].astype(F32) * value
 
+    def t_start(s):
+        each(chips - 1, lambda i: t_copy(s, i).start())
+
     each(bands - 1, tri_wait_same)
     local = t_make(c)
+    t_start(c)
     rdma(vir.at[c], vir.at[o], x_s.at[0], x_r.at[0], other, b).wait_recv()
     rdma(occ.at[c], occ.at[o], x_s.at[1], x_r.at[1], other, b).wait_recv()
     each(bands, tri_wait_cross)
     local = local + t_make(o)
-
-    def forward(i):
-        q = quarter ^ (i + 1)
-        rdma(piece(quarter, y), piece(q, y), ox_s.at[i], ox_r.at[q], mine, b).wait_recv()
-        each(side - 1, lambda n: occ_y(q, n).start())
-
-    each(3, forward)
-
-    def occ3(row):
-        return rdma(occ_c.at[c, :, :, row], occ_c.at[c, :, :, row], o3_s.at[row], o3_r.at[row], other, b)
-
-    occ3(y).start()
 
     high = local.astype(BF)
     low = (local - high.astype(F32)).astype(BF)
@@ -228,42 +230,46 @@
         return rdma(dens1.at[j], dens1.at[j], d1_s.at[i], d1_r.at[j], 2 * chip_peer(i) + c, b)
 
     each(chips - 1, lambda i: d1_copy(i).start())
+    t_start(o)
+
+    def forward(i):
+        q = quarter ^ (i + 1)
+        rdma(piece(quarter, y), piece(q, y), ox_s.at[i], ox_r.at[q], mine, b).wait_recv()
+        occ_y_start(q)
+
+    each(3, forward)
+
+    def occ3(row):
+        return rdma(occ_c.at[c, :, :, row], occ_c.at[c, :, :, row], o3_s.at[row], o3_r.at[row], other, b)
+
+    occ3(y).start()
+
     vir_t[o] = vir[o].T
-
-    loads[3].wait()
-
-    def widen(q):
-        k_f[q] = k_bf[q].astype(F32)
-
-    each(nk, widen)
-
-    def occ_rest(i):
-        row = lax.rem(y + 1 + i, side)
-        for q in range(4):
-            rdma(piece(q, row), piece(q, row), oy_s.at[q, i], oy_r.at[q, row], mine, b).wait_recv()
-        occ3(row).start()
-
-    each(side - 1, occ_rest)
-
-    def occ3_wait(row):
-        rdma(occ_c.at[c, :, :, row], occ_c.at[o, :, :, row], o3_s.at[row], o3_r.at[row], other, b).wait_recv()
-
-    each(side, occ3_wait)
-
-    def pairs_of(p):
-        for s in range(2):
-            points = occ_c[s, p].reshape(cols, nocc)
-            pairs[2 * p + s] = lax.dot_general(t_all[2 * p + s], points, ALONG, preferred_element_type=F32)
-
-    pairs_of(j)
-
-    def t_arrived(i):
-        p = chip_peer(i)
-        for s in range(2):
-            rdma(t_mine.at[0, s], t_all.at[2 * p + s], t_s.at[s, i], t_r.at[s, p], 2 * p + c, b).wait_recv()
-        pairs_of(p)
-
-    each(chips - 1, t_arrived)
+    turn[...] = jnp.zeros_like(turn)
+    loads[6].wait()
+    loads[7].wait()
+    turn[:, 0:width] = jnp.broadcast_to(vir_e[...], (nocc, width))
+    gaps = turn[...].T[0:width] - occ_e[...]
+    for v in range(2):
+        out[v] = gaps * trial[v]
+
+    def occ_near(i):
+        q = quarter ^ i
+        occ_y_wait(q, down)
+
+        @pl.when(q < 2)
+        def _():
+            occ_y(q, down, up, 2).start()
+
+        occ_y_wait(q, up)
+
+        @pl.when(q >= 2)
+        def _():
+            occ_y(q, up, down, 2).start()
+
+    each(4, occ_near)
+    occ3(down).start()
+    occ3(up).start()
 
     def d1_wait(i):
         p = chip_peer(i)
@@ -279,68 +285,23 @@
         return rdma(dens2.at[b], dens2.at[b], d2_s.at[i], d2_r.at[b], mine, band_peer(i))
 
     each(bands - 1, lambda i: d2_copy(i).start())
-    loads[4].wait()
-
-    tile = 16
-    fours = 4
-
-    def u_copy(dest, s):
-        return rdma(u_send.at[2 * dest + s], u_recv.at[j, s], u_s.at[s, dest], u_r.at[s, j], 2 * dest + c, b)
-
-    def screen(g, s):
-        dests = [j ^ (chips - 1 - fours * g - n) for n in range(fours)]
-
-        def rows_step(r):
-            part = block(r * tile, tile)
-            acc = [jnp.zeros((tile, cols), F32) for _ in dests]
-            for q in range(nk):
-                weight = k_f[q, part, :]
-                for n, dest in enumerate(dests):
-                    acc[n] = acc[n] + pairs[minus[2 * dest + s, q], part, :] * weight
-            for n in range(fours):
-                s_bf[n, part, :] = acc[n].astype(BF)
-
-        each(half // tile, rows_step)
-        for n, dest in enumerate(dests):
-            points = occ_c[s, dest].reshape(cols, nocc)
-            u_send[2 * dest + s] = jnp.dot(s_bf[n], points, preferred_element_type=F32).astype(BF)
-
-            @pl.when(dest != j)
-            def _():
-                u_copy(dest, s).start()
-
-    def finish(s):
-        mine_rows = block(h * half, half)
-        acc_w[s, mine_rows, :] = acc_w[s, mine_rows, :] - u_send[2 * j + s].astype(F32)
-
-        def u_arrived(i):
-            p = chip_peer(i)
-            rdma(u_send.at[2 * p + s], u_recv.at[p, s], u_s.at[s, p], u_r.at[s, p], 2 * p + c, b).wait_recv()
-            part = block((p // depth) * half, half)
-            acc_w[s, part, :] = acc_w[s, part, :] - u_recv[p, s].astype(F32)
-
-        each(chips - 1, u_arrived)
-        sig_send[s] = jnp.dot(vir_t[s], acc_w[s].astype(BF), preferred_element_type=F32).astype(BF)
-
-        def sig_start(p):
-            @pl.when((c != s) | (p != b))
-            def _():
-                sig_copy(s, p).start()
-
-        each(bands, sig_start)
-
-        @pl.when(c == s)
-        def _():
-            sig_recv[c, b] = sig_send[s, own_cols, :]
-
-    def sig_copy(s, p):
-        return rdma(
-            sig_send.at[s, block(p * width, width)], sig_recv.at[c, b], g_s.at[s, p], g_r.at[c, b], 2 * j + s, p
-        )
-
-    screen(0, 0)
-    screen(1, 0)
-    screen(0, 1)
+
+    each(4, lambda q: occ_y_wait(q, across))
+    occ3(across).start()
+
+    def pairs_of(p, s):
+        points = occ_c[s, p].reshape(cols, nocc)
+        k = 2 * p + s
+        pairs[k] = lax.dot_general(t_all[k], points, ALONG, preferred_element_type=F32).astype(BF)
+
+    def t_arrived(i):
+        p = chip_peer(i)
+        for s in range(2):
+            rdma(t_mine.at[0, s], t_all.at[2 * p + s], t_s.at[s, i], t_r.at[s, p], 2 * p + c, b).wait_recv()
+        pairs_of(p, c)
+
+    pairs_of(j, c)
+    each(chips - 1, t_arrived)
 
     def d2_wait(i):
         p = band_peer(i)
@@ -356,6 +317,74 @@
     for s in range(2):
         acc_w[s] = pot * occ[s].astype(F32)
 
+    def occ3_wait(row):
+        rdma(occ_c.at[c, :, :, row], occ_c.at[o, :, :, row], o3_s.at[row], o3_r.at[row], other, b).wait_recv()
+
+    each(side, occ3_wait)
+
+    each(chips, lambda p: pairs_of(p, o))
+    loads[3].wait()
+    loads[4].wait()
+
+    tile = 16
+    fours = 4
+
+    def u_copy(dest, s):
+        return rdma(u_send.at[2 * dest + s], u_recv.at[j, s], u_s.at[s, dest], u_r.at[s, j], 2 * dest + c, b)
+
+    def screen(g, s):
+        dests = [j ^ (chips - 1 - fours * g - n) for n in range(fours)]
+
+        def rows_step(r):
+            part = block(r * tile, tile)
+            for n, dest in enumerate(dests):
+                acc = jnp.zeros((tile, cols), F32)
+                for q in range(nk):
+                    acc = acc + pairs[minus[2 * dest + s, q], part, :].astype(F32) * k_bf[q, part, :].astype(F32)
+                s_bf[n, part, :] = acc.astype(BF)
+
+        each(half // tile, rows_step)
+        for n, dest in enumerate(dests):
+            points = occ_c[s, dest].reshape(cols, nocc)
+            u_send[2 * dest + s] = jnp.dot(s_bf[n], points, preferred_element_type=F32).astype(BF)
+
+            @pl.when(dest != j)
+            def _():
+                u_copy(dest, s).start()
+
+    def finish(s):
+        mine_rows = block(h * half, half)
+        acc_w[s, mine_rows, :] = acc_w[s, mine_rows, :] - u_send[2 * j + s].astype(F32)
+
+        def u_arrived(i):
+            p = chip_peer(i)
+            rdma(u_send.at[2 * p + s], u_recv.at[p, s], u_s.at[s, p], u_r.at[s, p], 2 * p + c, b).wait_recv()
+            part = block((p // depth) * half, half)
+            acc_w[s, part, :] = acc_w[s, part, :] - u_recv[p, s].astype(F32)
+
+        each(chips - 1, u_arrived)
+        sig_send[s] = jnp.dot(vir_t[s], acc_w[s].astype(BF), preferred_element_type=F32).astype(BF)
+
+        def sig_start(p):
+            @pl.when((c != s) | (p != b))
+            def _():
+                sig_copy(s, p).start()
+
+        each(bands, sig_start)
+
+        @pl.when(c == s)
+        def _():
+            sig_recv[c, b] = sig_send[s, own_cols, :]
+
+    def sig_copy(s, p):
+        return rdma(
+            sig_send.at[s, block(p * width, width)], sig_recv.at[c, b], g_s.at[s, p], g_r.at[c, b], 2 * j + s, p
+        )
+
+    screen(0, 0)
+    screen(1, 0)
+    screen(0, 1)
+
     finish(0)
     screen(1, 1)
     finish(1)
@@ -373,7 +402,7 @@
         sums = sig_recv[v, 0].astype(F32)
         for p in range(1, bands):
             sums = sums + sig_recv[v, p].astype(F32)
-        out[v] = sums
+        out[v] = out[v] + sums
 
     each(bands - 1, lambda i: tri_same(i).wait_send())
     each(bands, lambda i: tri_cross(i).wait_send())
@@ -388,7 +417,12 @@
     send_occ.wait_send()
     each(3, lambda i: occ_x(i).wait_send())
     for q in range(4):
-        each(side - 1, lambda i: occ_y(q, i).wait_send())
+        occ_y(q, y, up, 0).wait_send()
+        occ_y(q, y, down, 1).wait_send()
+        if q < 2:
+            occ_y(q, down, up, 2).wait_send()
+        else:
+            occ_y(q, up, down, 2).wait_send()
     each(side, lambda row: occ3(row).wait_send())
     each(chips - 1, lambda i: d1_copy(i).wait_send())
     each(bands - 1, lambda i: d2_copy(i).wait_send())
@@ -418,16 +452,19 @@
         turned = jnp.transpose(trial[0], (0, 2, 1))
         far = pl.BlockSpec(memory_space=pltpu.HBM)
         dma = pltpu.SemaphoreType.DMA
-        coupled = pl.pallas_call(
+        result = pl.pallas_call(
             kernel,
             out_shape=jax.ShapeDtypeStruct((2, width, nocc), F32),
-            in_specs=[far] * 6,
+            in_specs=[far] * 8,
             out_specs=pl.BlockSpec(memory_space=pltpu.VMEM),
             scratch_shapes=[
                 pltpu.SMEM((nk, nk), jnp.int32),
                 pltpu.VMEM((2, width, nocc), F32),
                 pltpu.VMEM((2, rows, nocc), BF),
                 pltpu.VMEM((2, rows, nvir), BF),
+                pltpu.VMEM((1, nocc), F32),
+                pltpu.VMEM((1, width), F32),
+                pltpu.VMEM((nocc, 128), F32),
                 pltpu.VMEM((2, width, nocc), BF),
                 pltpu.VMEM((2, nvir, nocc), BF),
                 pltpu.VMEM((2, nvir, rows), BF),
@@ -435,8 +472,7 @@
                 pltpu.VMEM((nk, half, nocc), BF),
                 pltpu.VMEM((2, chips, 4, bands // 2, rows // bands, nocc), BF),
                 pltpu.VMEM((nk, half, cols), BF),
-                pltpu.VMEM((nk, half, cols), F32),
-                pltpu.VMEM((nk, half, cols), F32),
+                pltpu.VMEM((nk, half, cols), BF),
                 pltpu.VMEM((4, half, cols), BF),
                 pltpu.VMEM((nk, half, nocc), BF),
                 pltpu.VMEM((chips, 2, half, nocc), BF),
@@ -450,22 +486,21 @@
                 dma((2,)), dma((2,)),
                 dma((bands,)), dma((chips,)),
                 dma((3,)), dma((4,)),
-                dma((4, bands // 2)), dma((4, bands // 2)),
+                dma((4, 3)), dma((4, bands // 2)),
                 dma((bands // 2,)), dma((bands // 2,)),
                 dma((2, chips)), dma((2, chips)),
                 dma((chips,)), dma((chips,)),
                 dma((bands,)), dma((bands,)),
                 dma((2, chips)), dma((2, chips)),
                 dma((2, bands)), dma((2, bands)),
-                dma((6,)),
+                dma((8,)),
             ],
             compiler_params=pltpu.CompilerParams(
                 collective_id=0, has_side_effects=True, vmem_limit_bytes=67043328
             ),
             name="sigma",
-        )(minus, turned, occ[0], vir[0], coulomb, exch)
-        gaps = vir_energy[0][None, :] - occ_energy[0][:, None]
-        return (gaps[None] * trial[0] + jnp.transpose(coupled, (0, 2, 1)))[None]
+        )(minus, turned, occ[0], vir[0], coulomb, exch, occ_energy, vir_energy)
+        return jnp.transpose(result, (0, 2, 1))[None]
 
     in_specs = (
         P("ka", "band", None),

time: 60.1 us -> 59.1 us (0.983)
  other arithmetic: 3 us -> 0 us
  local copies, waits for them, and re-layouts: 0 us -> 1.55 us
    broadcast_in_dim x1 -> x0, other arithmetic: 1.62 us -> none  [per_device(): return (gaps[None] * trial[0] + jnp.transpose(coupled, (0, 2, 1)))[None]]
    unnamed x0 -> x1, local copies, waits for them, and re-layouts: none -> 1.55 us
    sub x1 -> x0, other arithmetic: 1.38 us -> none  [per_device(): gaps = vir_energy[0][None, :] - occ_energy[0][:, None]]
where the time goes in v3:
time: 59.1 us; the launch traced here: 58.9 us
  Pallas kernels  57.4 us (97%)
  local copies, waits for them, and re-layouts  1.55 us (3%)
    pallas_call x1, Pallas kernels, per_device(): pl.pallas_call(kernel, out_shape=jax.ShapeDtypeStruct((2, width, nocc), F...  57.4 us
    unnamed x1, local copies, waits for them, and re-layouts  1.55 us

profile of v3, /device:TPU:1, one launch (start us, length us, event | category | flops | bytes accessed | tf_op | source)
XLA Modules:
  0.0 58.9 jit_solution(13640840060106912805)
XLA Ops:
  0.0 57.4 %sigma.1 = f32[2,112,128]{2,1,0:T(8,128)} custom-call(s32[16,16]{1,0:T(8,128)} %minus_h.1, f32[2,112,128]{2,1,0:T(8,128)} %bitcast.10, bf16[256,128]{1,0:T(8,128)(2,1)} %bitcast.11, bf16[256,896]{1,0:T(8,128)(2,1)} %bitcast.8, bf16[256,2048]{1,0:T(8,128)(2,1)} %coulomb.1, bf16[16,256,2048]{2,1,0:T(8,128)(2,1)} %exch.1, f32[1,128]{1,0:T(1,128)} %occ_e_h.1, ...), custom_call_target="tpu_custom_call" | custom-call | tf_op jit(solution)/shard_map/sigma/pallas_call | solution.py:455
  57.4 1.6 %copy.10 = f32[1,2,128,112]{2,3,1,0:T(8,128)} copy(f32[1,2,128,112]{2,3,1,0:T(8,128)} %bitcast.9) | data formatting | bytes 229376

commit v4 on v3

--- a/solution.py
+++ b/solution.py
@@ -34,7 +34,7 @@
     minus_h, trial_h, occ_h, vir_h, coulomb, exch, occ_e_h, vir_e_h, out,
     minus, trial, occ, vir, occ_e, vir_e, turn, trial_bf, trial_all, vir_t, t_mine, t_all, occ_c, k_bf, pairs, s_bf,
     u_send, u_recv, acc_w, dens1, dens2, coul, sig_send, sig_recv,
-    tri_s, tri_r, x_s, x_r, o1_s, o1_r, ox_s, ox_r, oy_s, oy_r, o3_s, o3_r, t_s, t_r, d1_s, d1_r, d2_s, d2_r,
+    tri_s, tri_r, x_s, x_r, o1_s, o1_r, ox_s, ox_r, oy_s, oy_r, fy_s, fy_r, fx_s, fx_r, o3_s, o3_r, t_s, f_s, t_r, d1_s, d1_r, d2_s, d2_r,
     u_s, u_r, g_s, g_r, loc,
 ):
     bands = lax.axis_size("band")
@@ -57,10 +57,11 @@
     half = rows // 2
     width = trial.shape[1]
     nk = exch.shape[0]
-    slab = rows // bands
+    slab = rows // side
     cols = pairs.shape[2]
-    home = 2 * z + h
-    goal = lax.rem(b, 2) * depth + b // 2
+    home = xl * side + z
+    goal = h * depth + y
+    partner = (1 - h) * depth + z
 
     def band_peer(i):
         return lax.rem(b + 1 + i, bands)
@@ -76,7 +77,11 @@
         pltpu.make_async_copy(trial_h, trial, loc.at[1]),
         pltpu.make_async_copy(vir_h, vir.at[c], loc.at[2]),
         pltpu.make_async_copy(
-            exch.at[:, block(h * half, half), block(z * cols, cols, 128)], k_bf, loc.at[3]
+            exch.at[:, block(h * half, half), block(z * rows, rows, 128)], k_bf.at[:, :, pl.ds(0, rows)], loc.at[3]
+        ),
+        pltpu.make_async_copy(
+            exch.at[:, block(h * half, half), block((z + side) * rows, rows, 128)],
+            k_bf.at[:, :, pl.ds(rows, rows)], loc.at[8],
         ),
         pltpu.make_async_copy(minus_h, minus, loc.at[4]),
         pltpu.make_async_copy(coulomb, coul, loc.at[5]),
@@ -95,42 +100,37 @@
         greet(mine, band_peer(i))
         greet(other, band_peer(i))
 
-    def greet_chip(i):
-        greet(2 * chip_peer(i) + c, b)
-        greet(2 * chip_peer(i) + c, home)
+    def deep(i):
+        return h * depth + lax.rem(z + 1 + i, depth)
 
     each(bands - 1, greet_band)
-    each(chips - 1, greet_chip)
+    each(chips - 1, lambda i: greet(2 * chip_peer(i) + c, b))
+    each(depth - 1, lambda i: greet(2 * deep(i) + c, home))
     greet(other, b)
     greet(2 * ((1 - h) * depth + z) + c, (1 - xl) * side + y)
-
-    @pl.when(home != b)
-    def _():
-        greet(mine, home)
 
     loads[0].wait()
     loads[1].wait()
     trial_bf[...] = trial[...].astype(BF)
-    callers = 2 * (bands - 1) + 2 * (chips - 1) + 2
-    pl.semaphore_wait(barrier, jnp.where(home == b, callers, callers + 1))
+    callers = 2 * (bands - 1) + (chips - 1) + 2
+    pl.semaphore_wait(barrier, jnp.where(y == z, callers, callers + side))
 
     def occ1(i):
         return rdma(
-            occ.at[c, block(i * slab, slab)],
-            occ_c.at[c, j, 2 * lax.rem(b, 2) + i // side, lax.rem(i, side)],
-            o1_s.at[i], o1_r.at[j], 2 * goal + c, i,
+            occ.at[c, block(i * slab, slab)], occ_c.at[c, quarter, z, i], o1_s.at[i], o1_r.at[z],
+            2 * goal + c, xl * side + i,
         )
 
     def occ1_start(i):
-        @pl.when((i != b) | (goal != j))
+        @pl.when((i != y) | (y != z))
         def _():
             occ1(i).start()
 
-    each(bands, occ1_start)
-
-    @pl.when(home == b)
+    each(side, occ1_start)
+
+    @pl.when(y == z)
     def _():
-        occ_c[c, j, quarter, y] = occ[c, block(b * slab, slab), :]
+        occ_c[c, quarter, z, y] = occ[c, block(y * slab, slab), :]
 
     own_cols = block(b * width, width)
 
@@ -151,40 +151,47 @@
     trial_all[c, own_cols, :] = trial_bf[c]
 
     def occ1_wait(i):
-        @pl.when((i != j) | (home != b))
+        @pl.when((i != z) | (y != z))
         def _():
             rdma(
-                occ.at[c, block(b * slab, slab)], occ_c.at[c, i, quarter, y], o1_s.at[i], o1_r.at[i], mine, b
+                occ.at[c, block(y * slab, slab)], occ_c.at[c, quarter, i, y], o1_s.at[0], o1_r.at[i], mine, b
             ).wait_recv()
 
-    each(chips, occ1_wait)
+    each(depth, occ1_wait)
 
     def piece(q, row):
-        return occ_c.at[c, :, q, row]
+        return occ_c.at[c, q, :, row]
+
+    def part_a(q, row):
+        return occ_c.at[c, q, pl.ds(0, depth // 2), row]
+
+    def part_b(q, row):
+        return occ_c.at[c, q, pl.ds(depth // 2, depth // 2), row]
+
+    def x_send(src, send, recv, i):
+        q = quarter ^ (i + 1)
+        return rdma(src, src, send, recv, 2 * ((q // 2) * depth + z) + c, lax.rem(q, 2) * side + y)
+
+    def y_send(src, send, recv, i):
+        return rdma(src, src, send, recv, mine, xl * side + lax.rem(y + 1 + i, side))
 
     def occ_x(i):
-        q = quarter ^ (i + 1)
-        return rdma(
-            piece(quarter, y), piece(quarter, y), ox_s.at[i], ox_r.at[quarter],
-            2 * ((q // 2) * depth + z) + c, lax.rem(q, 2) * side + y,
-        )
-
-    up = lax.rem(y + 1, side)
-    down = lax.rem(y + side - 1, side)
-    across = lax.rem(y + 2, side)
-
-    def occ_y(q, row, to, n):
-        return rdma(piece(q, row), piece(q, row), oy_s.at[q, n], oy_r.at[q, row], mine, xl * side + to)
-
-    def occ_y_start(q):
-        occ_y(q, y, up, 0).start()
-        occ_y(q, y, down, 1).start()
-
-    def occ_y_wait(q, row):
-        rdma(piece(q, row), piece(q, row), oy_s.at[q, 0], oy_r.at[q, row], mine, b).wait_recv()
+        return x_send(piece(quarter, y), ox_s.at[i], ox_r.at[quarter], i)
+
+    def occ_y(i):
+        return y_send(piece(quarter, y), oy_s.at[i], oy_r.at[y], i)
+
+    def occ_xy(q, i):
+        return y_send(part_a(q, y), fy_s.at[q, i], fy_r.at[q, y], i)
+
+    def occ_yx(row, i):
+        return x_send(part_b(quarter, row), fx_s.at[row, i], fx_r.at[quarter, row], i)
+
+    def landed(dst, recv):
+        rdma(dst, dst, x_s.at[0], recv, mine, b).wait_recv()
 
     each(3, lambda i: occ_x(i).start())
-    occ_y_start(quarter)
+    each(side - 1, lambda i: occ_y(i).start())
 
     vir_t[c] = vir[c].T
 
@@ -198,8 +205,19 @@
         rdma(trial_bf.at[o], trial_all.at[o, part], tri_s.at[1, i], tri_r.at[o, i], other, i).wait_recv()
 
     def t_copy(s, i):
-        p = chip_peer(i)
-        return rdma(t_mine.at[p // depth, s], t_all.at[2 * j + s], t_s.at[s, i], t_r.at[s, j], 2 * p + c, b)
+        return rdma(t_mine.at[h, s], t_all.at[2 * j + s], t_s.at[s, i], t_r.at[s, j], 2 * deep(i) + c, b)
+
+    def t_cross(s):
+        return rdma(
+            t_mine.at[1 - h, s], t_all.at[2 * j + s], t_s.at[s, depth - 1], t_r.at[s, j], 2 * partner + c, b
+        )
+
+    def t_forward(s, i):
+        there = t_all.at[2 * partner + s]
+        return rdma(there, there, f_s.at[s, i], t_r.at[s, partner], 2 * deep(i) + c, b)
+
+    def t_landed(s, p):
+        landed(t_all.at[2 * p + s], t_r.at[s, p])
 
     def t_make(s):
         value = jnp.dot(vir[s], trial_all[s], preferred_element_type=F32)
@@ -209,7 +227,8 @@
         return occ[s].astype(F32) * value
 
     def t_start(s):
-        each(chips - 1, lambda i: t_copy(s, i).start())
+        t_cross(s).start()
+        each(depth - 1, lambda i: t_copy(s, i).start())
 
     each(bands - 1, tri_wait_same)
     local = t_make(c)
@@ -232,44 +251,60 @@
     each(chips - 1, lambda i: d1_copy(i).start())
     t_start(o)
 
-    def forward(i):
+    def x_arrived(i):
         q = quarter ^ (i + 1)
-        rdma(piece(quarter, y), piece(q, y), ox_s.at[i], ox_r.at[q], mine, b).wait_recv()
-        occ_y_start(q)
-
-    each(3, forward)
-
-    def occ3(row):
-        return rdma(occ_c.at[c, :, :, row], occ_c.at[c, :, :, row], o3_s.at[row], o3_r.at[row], other, b)
-
-    occ3(y).start()
+        landed(piece(q, y), ox_r.at[q])
+        each(side - 1, lambda n: occ_xy(q, n).start())
+
+    def y_arrived(i):
+        row = lax.rem(y + 1 + i, side)
+        landed(piece(quarter, row), oy_r.at[row])
+        each(3, lambda n: occ_yx(row, n).start())
+
+    each(3, x_arrived)
+    each(side - 1, y_arrived)
+
+    def t_pass(s):
+        t_landed(s, partner)
+        each(depth - 1, lambda i: t_forward(s, i).start())
+
+    t_pass(c)
+    t_pass(o)
+
+    def occ3(n):
+        q = quarter ^ (n // 2)
+        there = occ_c.at[c, q, pl.ds(lax.rem(n, 2) * (depth // 2), depth // 2)]
+        return rdma(there, there, o3_s.at[n], o3_r.at[n], other, b)
+
+    occ3(0).start()
+    occ3(1).start()
 
     vir_t[o] = vir[o].T
     turn[...] = jnp.zeros_like(turn)
-    loads[6].wait()
     loads[7].wait()
+    loads[8].wait()
     turn[:, 0:width] = jnp.broadcast_to(vir_e[...], (nocc, width))
     gaps = turn[...].T[0:width] - occ_e[...]
     for v in range(2):
         out[v] = gaps * trial[v]
 
-    def occ_near(i):
-        q = quarter ^ i
-        occ_y_wait(q, down)
-
-        @pl.when(q < 2)
-        def _():
-            occ_y(q, down, up, 2).start()
-
-        occ_y_wait(q, up)
-
-        @pl.when(q >= 2)
-        def _():
-            occ_y(q, up, down, 2).start()
-
-    each(4, occ_near)
-    occ3(down).start()
-    occ3(up).start()
+    def occ_rest(i):
+        q = quarter ^ (i + 1)
+
+        def from_y(n):
+            row = lax.rem(y + 1 + n, side)
+            landed(part_a(q, row), fy_r.at[q, row])
+
+        def from_x(n):
+            row = lax.rem(y + 1 + n, side)
+            landed(part_b(q, row), fx_r.at[q, row])
+
+        each(side - 1, from_y)
+        occ3(2 * i + 2).start()
+        each(side - 1, from_x)
+        occ3(2 * i + 3).start()
+
+    each(3, occ_rest)
 
     def d1_wait(i):
         p = chip_peer(i)
@@ -286,29 +321,33 @@
 
     each(bands - 1, lambda i: d2_copy(i).start())
 
-    each(4, lambda q: occ_y_wait(q, across))
-    occ3(across).start()
-
-    def pairs_of(p, s):
-        points = occ_c[s, p].reshape(cols, nocc)
-        k = 2 * p + s
-        pairs[k] = lax.dot_general(t_all[k], points, ALONG, preferred_element_type=F32).astype(BF)
-
-    def t_arrived(i):
-        p = chip_peer(i)
+    def t_rest(i):
+        near = deep(i)
+        far = lax.rem(near + depth, chips)
         for s in range(2):
-            rdma(t_mine.at[0, s], t_all.at[2 * p + s], t_s.at[s, i], t_r.at[s, p], 2 * p + c, b).wait_recv()
-        pairs_of(p, c)
-
-    pairs_of(j, c)
-    each(chips - 1, t_arrived)
+            t_landed(s, near)
+            t_landed(s, far)
+
+    each(depth - 1, t_rest)
+
+    def points_of(p, s, e):
+        return occ_c[s, 2 * (p // depth) + e, lax.rem(p, depth)].reshape(rows, nocc)
+
+    def pairs_of(s):
+        for p in range(chips):
+            for e in range(2):
+                pairs[2 * p + s, :, e * rows : (e + 1) * rows] = lax.dot_general(
+                    t_all[2 * p + s], points_of(p, s, e), ALONG, preferred_element_type=F32
+                ).astype(BF)
+
+    pairs_of(c)
 
     def d2_wait(i):
         p = band_peer(i)
         rdma(dens2.at[p], dens2.at[p], d2_s.at[i], d2_r.at[p], mine, p).wait_recv()
 
     each(bands - 1, d2_wait)
-    loads[5].wait()
+    loads[6].wait()
     pot = jnp.zeros((rows, nocc), F32)
     for p in range(bands):
         line = jnp.broadcast_to(dens2[p][0:1, :].astype(BF), (nocc, rows))
@@ -317,14 +356,16 @@
     for s in range(2):
         acc_w[s] = pot * occ[s].astype(F32)
 
-    def occ3_wait(row):
-        rdma(occ_c.at[c, :, :, row], occ_c.at[o, :, :, row], o3_s.at[row], o3_r.at[row], other, b).wait_recv()
-
-    each(side, occ3_wait)
-
-    each(chips, lambda p: pairs_of(p, o))
+    def occ3_wait(n):
+        q = quarter ^ (n // 2)
+        landed(occ_c.at[o, q, pl.ds(lax.rem(n, 2) * (depth // 2), depth // 2)], o3_r.at[n])
+
+    each(8, occ3_wait)
+
+    pairs_of(o)
     loads[3].wait()
     loads[4].wait()
+    loads[5].wait()
 
     tile = 16
     fours = 4
@@ -345,8 +386,9 @@
 
         each(half // tile, rows_step)
         for n, dest in enumerate(dests):
-            points = occ_c[s, dest].reshape(cols, nocc)
-            u_send[2 * dest + s] = jnp.dot(s_bf[n], points, preferred_element_type=F32).astype(BF)
+            part_sum = jnp.dot(s_bf[n, :, :rows], points_of(dest, s, 0), preferred_element_type=F32)
+            part_sum = part_sum + jnp.dot(s_bf[n, :, rows:], points_of(dest, s, 1), preferred_element_type=F32)
+            u_send[2 * dest + s] = part_sum.astype(BF)
 
             @pl.when(dest != j)
             def _():
@@ -385,8 +427,8 @@
     screen(1, 0)
     screen(0, 1)
 
+    screen(1, 1)
     finish(0)
-    screen(1, 1)
     finish(1)
 
     def sig_wait_same(i):
@@ -408,26 +450,28 @@
     each(bands, lambda i: tri_cross(i).wait_send())
 
     def occ1_sent(i):
-        @pl.when((i != b) | (goal != j))
+        @pl.when((i != y) | (y != z))
         def _():
             occ1(i).wait_send()
 
-    each(bands, occ1_sent)
+    each(side, occ1_sent)
     send_vir.wait_send()
     send_occ.wait_send()
     each(3, lambda i: occ_x(i).wait_send())
-    for q in range(4):
-        occ_y(q, y, up, 0).wait_send()
-        occ_y(q, y, down, 1).wait_send()
-        if q < 2:
-            occ_y(q, down, up, 2).wait_send()
-        else:
-            occ_y(q, up, down, 2).wait_send()
-    each(side, lambda row: occ3(row).wait_send())
+    each(side - 1, lambda i: occ_y(i).wait_send())
+
+    def forwarded(i):
+        each(side - 1, lambda n: occ_xy(quarter ^ (i + 1), n).wait_send())
+        each(3, lambda n: occ_yx(lax.rem(y + 1 + i, side), n).wait_send())
+
+    each(3, forwarded)
+    each(8, lambda n: occ3(n).wait_send())
     each(chips - 1, lambda i: d1_copy(i).wait_send())
     each(bands - 1, lambda i: d2_copy(i).wait_send())
     for s in range(2):
-        each(chips - 1, lambda i: t_copy(s, i).wait_send())
+        each(depth - 1, lambda i: t_copy(s, i).wait_send())
+        t_cross(s).wait_send()
+        each(depth - 1, lambda i: t_forward(s, i).wait_send())
         each(chips - 1, lambda i: u_copy(chip_peer(i), s).wait_send())
 
         def sig_sent(p):
@@ -470,7 +514,7 @@
                 pltpu.VMEM((2, nvir, rows), BF),
                 pltpu.VMEM((2, 2, half, nocc), BF),
                 pltpu.VMEM((nk, half, nocc), BF),
-                pltpu.VMEM((2, chips, 4, bands // 2, rows // bands, nocc), BF),
+                pltpu.VMEM((2, 4, chips // 2, bands // 2, 2 * rows // bands, nocc), BF),
                 pltpu.VMEM((nk, half, cols), BF),
                 pltpu.VMEM((nk, half, cols), BF),
                 pltpu.VMEM((4, half, cols), BF),
@@ -484,16 +528,18 @@
                 pltpu.VMEM((2, bands, width, nocc), BF),
                 dma((2, bands)), dma((2, bands)),
                 dma((2,)), dma((2,)),
-                dma((bands,)), dma((chips,)),
+                dma((bands // 2,)), dma((chips // 2,)),
                 dma((3,)), dma((4,)),
+                dma((3,)), dma((bands // 2,)),
                 dma((4, 3)), dma((4, bands // 2)),
-                dma((bands // 2,)), dma((bands // 2,)),
-                dma((2, chips)), dma((2, chips)),
+                dma((bands // 2, 3)), dma((4, bands // 2)),
+                dma((8,)), dma((8,)),
+                dma((2, 4)), dma((2, 4)), dma((2, chips)),
                 dma((chips,)), dma((chips,)),
                 dma((bands,)), dma((bands,)),
                 dma((2, chips)), dma((2, chips)),
                 dma((2, bands)), dma((2, bands)),
-                dma((8,)),
+                dma((9,)),
             ],
             compiler_params=pltpu.CompilerParams(
                 collective_id=0, has_side_effects=True, vmem_limit_bytes=67043328

time: 59.1 us -> 53.5 us (0.905)
  Pallas kernels: 57.4 us -> 51.8 us
    pallas_call x1, Pallas kernels: 57.4 us -> 51.8 us  [per_device(): pl.pallas_call(kernel, out_shape=jax.ShapeDtypeStruct((2, width, nocc), F...]
where the time goes in v4:
time: 53.5 us; the launch traced here: 53.4 us
  Pallas kernels  51.8 us (97%)
  local copies, waits for them, and re-layouts  1.55 us (3%)
    pallas_call x1, Pallas kernels, per_device(): pl.pallas_call(kernel, out_shape=jax.ShapeDtypeStruct((2, width, nocc), F...  51.8 us
    unnamed x1, local copies, waits for them, and re-layouts  1.55 us

profile of v4, /device:TPU:1, one launch (start us, length us, event | category | flops | bytes accessed | tf_op | source)
XLA Modules:
  0.0 53.4 jit_solution(10660103253333647161)
XLA Ops:
  0.0 51.8 %sigma.1 = f32[2,112,128]{2,1,0:T(8,128)} custom-call(s32[16,16]{1,0:T(8,128)} %minus_h.1, f32[2,112,128]{2,1,0:T(8,128)} %bitcast.10, bf16[256,128]{1,0:T(8,128)(2,1)} %bitcast.11, bf16[256,896]{1,0:T(8,128)(2,1)} %bitcast.8, bf16[256,2048]{1,0:T(8,128)(2,1)} %coulomb.1, bf16[16,256,2048]{2,1,0:T(8,128)(2,1)} %exch.1, f32[1,128]{1,0:T(1,128)} %occ_e_h.1, ...), custom_call_target="tpu_custom_call" | custom-call | tf_op jit(solution)/shard_map/sigma/pallas_call | solution.py:499
  51.8 1.6 %copy.10 = f32[1,2,128,112]{2,3,1,0:T(8,128)} copy(f32[1,2,128,112]{2,3,1,0:T(8,128)} %bitcast.9) | data formatting | bytes 229376

commit v5 on v4

--- a/solution.py
+++ b/solution.py
@@ -342,6 +342,79 @@
 
     pairs_of(c)
 
+    def occ3_wait(n):
+        q = quarter ^ (n // 2)
+        landed(occ_c.at[o, q, pl.ds(lax.rem(n, 2) * (depth // 2), depth // 2)], o3_r.at[n])
+
+    each(8, occ3_wait)
+
+    pairs_of(o)
+    loads[3].wait()
+    loads[4].wait()
+    loads[5].wait()
+
+    tile = 16
+    fours = 4
+
+    def u_copy(dest, s):
+        return rdma(u_send.at[2 * dest + s], u_recv.at[j, s], u_s.at[s, dest], u_r.at[s, j], 2 * dest + c, b)
+
+    def screen(g, s):
+        dests = [j ^ (chips - 1 - fours * g - n) for n in range(fours)]
+
+        def rows_step(r):
+            part = block(r * tile, tile)
+            for n, dest in enumerate(dests):
+                acc = jnp.zeros((tile, cols), F32)
+                for q in range(nk):
+                    acc = acc + pairs[minus[2 * dest + s, q], part, :].astype(F32) * k_bf[q, part, :].astype(F32)
+                s_bf[n, part, :] = acc.astype(BF)
+
+        each(half // tile, rows_step)
+        sums = []
+        for n, dest in enumerate(dests):
+            left = jnp.dot(s_bf[n, :, :rows], points_of(dest, s, 0), preferred_element_type=F32)
+            sums.append(left + jnp.dot(s_bf[n, :, rows:], points_of(dest, s, 1), preferred_element_type=F32))
+        for n, dest in enumerate(dests):
+            u_send[2 * dest + s] = sums[n].astype(BF)
+        for n, dest in enumerate(dests):
+            if chips - 1 - fours * g - n:
+                u_copy(dest, s).start()
+
+    def finish(s):
+        mine_rows = block(h * half, half)
+        acc_w[s, mine_rows, :] = acc_w[s, mine_rows, :] - u_send[2 * j + s].astype(F32)
+
+        def u_arrived(i):
+            p = chip_peer(i)
+            rdma(u_send.at[2 * p + s], u_recv.at[p, s], u_s.at[s, p], u_r.at[s, p], 2 * p + c, b).wait_recv()
+            part = block((p // depth) * half, half)
+            acc_w[s, part, :] = acc_w[s, part, :] - u_recv[p, s].astype(F32)
+
+        each(chips - 1, u_arrived)
+        sig_send[s] = jnp.dot(vir_t[s], acc_w[s].astype(BF), preferred_element_type=F32).astype(BF)
+
+        def sig_start(p):
+            @pl.when((c != s) | (p != b))
+            def _():
+                sig_copy(s, p).start()
+
+        each(bands, sig_start)
+
+        @pl.when(c == s)
+        def _():
+            sig_recv[c, b] = sig_send[s, own_cols, :]
+
+    def sig_copy(s, p):
+        return rdma(
+            sig_send.at[s, block(p * width, width)], sig_recv.at[c, b], g_s.at[s, p], g_r.at[c, b], 2 * j + s, p
+        )
+
+    screen(0, 0)
+    screen(1, 0)
+    screen(0, 1)
+
+    screen(1, 1)
     def d2_wait(i):
         p = band_peer(i)
         rdma(dens2.at[p], dens2.at[p], d2_s.at[i], d2_r.at[p], mine, p).wait_recv()
@@ -356,96 +429,7 @@
     for s in range(2):
         acc_w[s] = pot * occ[s].astype(F32)
 
-    def occ3_wait(n):
-        q = quarter ^ (n // 2)
-        landed(occ_c.at[o, q, pl.ds(lax.rem(n, 2) * (depth // 2), depth // 2)], o3_r.at[n])
-
-    each(8, occ3_wait)
-
-    pairs_of(o)
-    loads[3].wait()
-    loads[4].wait()
-    loads[5].wait()
-
-    tile = 16
-    fours = 4
-
-    def u_copy(dest, s):
-        return rdma(u_send.at[2 * dest + s], u_recv.at[j, s], u_s.at[s, dest], u_r.at[s, j], 2 * dest + c, b)
-
-    def screen(g, s):
-        dests = [j ^ (chips - 1 - fours * g - n) for n in range(fours)]
-
-        def rows_step(r):
-            part = block(r * tile, tile)
-            for n, dest in enumerate(dests):
-                acc = jnp.zeros((tile, cols), F32)
-                for q in range(nk):
-                    acc = acc + pairs[minus[2 * dest + s, q], part, :].astype(F32) * k_bf[q, part, :].astype(F32)
-                s_bf[n, part, :] = acc.astype(BF)
-
-        each(half // tile, rows_step)
-        for n, dest in enumerate(dests):
-            part_sum = jnp.dot(s_bf[n, :, :rows], points_of(dest, s, 0), preferred_element_type=F32)
-            part_sum = part_sum + jnp.dot(s_bf[n, :, rows:], points_of(dest, s, 1), preferred_element_type=F32)
-            u_send[2 * dest + s] = part_sum.astype(BF)
-
-            @pl.when(dest != j)
-            def _():
-                u_copy(dest, s).start()
-
-    def finish(s):
-        mine_rows = block(h * half, half)
-        acc_w[s, mine_rows, :] = acc_w[s, mine_rows, :] - u_send[2 * j + s].astype(F32)
-
-        def u_arrived(i):
-            p = chip_peer(i)
-            rdma(u_send.at[2 * p + s], u_recv.at[p, s], u_s.at[s, p], u_r.at[s, p], 2 * p + c, b).wait_recv()
-            part = block((p // depth) * half, half)
-            acc_w[s, part, :] = acc_w[s, part, :] - u_recv[p, s].astype(F32)
-
-        each(chips - 1, u_arrived)
-        sig_send[s] = jnp.dot(vir_t[s], acc_w[s].astype(BF), preferred_element_type=F32).astype(BF)
-
-        def sig_start(p):
-            @pl.when((c != s) | (p != b))
-            def _():
-                sig_copy(s, p).start()
-
-        each(bands, sig_start)
-
-        @pl.when(c == s)
-        def _():
-            sig_recv[c, b] = sig_send[s, own_cols, :]
-
-    def sig_copy(s, p):
-        return rdma(
-            sig_send.at[s, block(p * width, width)], sig_recv.at[c, b], g_s.at[s, p], g_r.at[c, b], 2 * j + s, p
-        )
-
-    screen(0, 0)
-    screen(1, 0)
-    screen(0, 1)
-
-    screen(1, 1)
     finish(0)
-    finish(1)
-
-    def sig_wait_same(i):
-        p = band_peer(i)
-        rdma(sig_send.at[0, own_cols], sig_recv.at[c, p], g_s.at[0, i], g_r.at[c, p], mine, p).wait_recv()
-
-    def sig_wait_cross(i):
-        rdma(sig_send.at[0, own_cols], sig_recv.at[o, i], g_s.at[1, i], g_r.at[o, i], other, i).wait_recv()
-
-    each(bands - 1, sig_wait_same)
-    each(bands, sig_wait_cross)
-    for v in range(2):
-        sums = sig_recv[v, 0].astype(F32)
-        for p in range(1, bands):
-            sums = sums + sig_recv[v, p].astype(F32)
-        out[v] = out[v] + sums
-
     each(bands - 1, lambda i: tri_same(i).wait_send())
     each(bands, lambda i: tri_cross(i).wait_send())
 
@@ -472,6 +456,25 @@
         each(depth - 1, lambda i: t_copy(s, i).wait_send())
         t_cross(s).wait_send()
         each(depth - 1, lambda i: t_forward(s, i).wait_send())
+
+    finish(1)
+
+    def sig_wait_same(i):
+        p = band_peer(i)
+        rdma(sig_send.at[0, own_cols], sig_recv.at[c, p], g_s.at[0, i], g_r.at[c, p], mine, p).wait_recv()
+
+    def sig_wait_cross(i):
+        rdma(sig_send.at[0, own_cols], sig_recv.at[o, i], g_s.at[1, i], g_r.at[o, i], other, i).wait_recv()
+
+    each(bands - 1, sig_wait_same)
+    each(bands, sig_wait_cross)
+    for v in range(2):
+        sums = sig_recv[v, 0].astype(F32)
+        for p in range(1, bands):
+            sums = sums + sig_recv[v, p].astype(F32)
+        out[v] = out[v] + sums
+
+    for s in range(2):
         each(chips - 1, lambda i: u_copy(chip_peer(i), s).wait_send())
 
         def sig_sent(p):

time: 53.5 us -> 49.4 us (0.923)
  Pallas kernels: 51.8 us -> 47.6 us
    pallas_call x1, Pallas kernels: 51.8 us -> 47.6 us  [per_device(): pl.pallas_call(kernel, out_shape=jax.ShapeDtypeStruct((2, width, nocc), F...]
where the time goes in v5:
time: 49.4 us; the launch traced here: 49.1 us
  Pallas kernels  47.6 us (96%)
  local copies, waits for them, and re-layouts  1.55 us (3%)
    pallas_call x1, Pallas kernels, per_device(): pl.pallas_call(kernel, out_shape=jax.ShapeDtypeStruct((2, width, nocc), F...  47.6 us
    unnamed x1, local copies, waits for them, and re-layouts  1.55 us

profile of v5, /device:TPU:1, one launch (start us, length us, event | category | flops | bytes accessed | tf_op | source)
XLA Modules:
  0.0 49.1 jit_solution(9524138899973012845)
XLA Ops:
  0.0 47.6 %sigma.1 = f32[2,112,128]{2,1,0:T(8,128)} custom-call(s32[16,16]{1,0:T(8,128)} %minus_h.1, f32[2,112,128]{2,1,0:T(8,128)} %bitcast.10, bf16[256,128]{1,0:T(8,128)(2,1)} %bitcast.11, bf16[256,896]{1,0:T(8,128)(2,1)} %bitcast.8, bf16[256,2048]{1,0:T(8,128)(2,1)} %coulomb.1, bf16[16,256,2048]{2,1,0:T(8,128)(2,1)} %exch.1, f32[1,128]{1,0:T(1,128)} %occ_e_h.1, ...), custom_call_target="tpu_custom_call" | custom-call | tf_op jit(solution)/shard_map/sigma/pallas_call | solution.py:502
  47.6 1.6 %copy.10 = f32[1,2,128,112]{2,3,1,0:T(8,128)} copy(f32[1,2,128,112]{2,3,1,0:T(8,128)} %bitcast.9) | data formatting | bytes 229376

commit v6 on v5

--- a/solution.py
+++ b/solution.py
@@ -34,7 +34,7 @@
     minus_h, trial_h, occ_h, vir_h, coulomb, exch, occ_e_h, vir_e_h, out,
     minus, trial, occ, vir, occ_e, vir_e, turn, trial_bf, trial_all, vir_t, t_mine, t_all, occ_c, k_bf, pairs, s_bf,
     u_send, u_recv, acc_w, dens1, dens2, coul, sig_send, sig_recv,
-    tri_s, tri_r, x_s, x_r, o1_s, o1_r, ox_s, ox_r, oy_s, oy_r, fy_s, fy_r, fx_s, fx_r, o3_s, o3_r, t_s, f_s, t_r, d1_s, d1_r, d2_s, d2_r,
+    tri_s, tri_r, tri_f, x_s, x_r, o1_s, o1_r, ox_s, ox_r, oy_s, oy_r, fy_s, fy_r, fx_s, fx_r, o3_s, o3_r, t_s, f_s, t_r, d1_s, d1_r, d2_s, d2_r,
     u_s, u_r, g_s, g_r, loc,
 ):
     bands = lax.axis_size("band")
@@ -134,21 +134,51 @@
 
     own_cols = block(b * width, width)
 
-    def tri_same(i):
-        return rdma(trial_bf.at[c], trial_all.at[c, own_cols], tri_s.at[0, i], tri_r.at[c, b], mine, band_peer(i))
-
-    def tri_cross(i):
-        p = lax.rem(b + i, bands)
-        return rdma(trial_bf.at[o], trial_all.at[c, own_cols], tri_s.at[1, i], tri_r.at[c, b], other, p)
-
-    each(bands - 1, lambda i: tri_same(i).start())
+    facing = (1 - xl) * side + y
+
+    def beside(i):
+        return xl * side + lax.rem(y + 1 + i, side)
+
+    def behind(i):
+        return (1 - xl) * side + lax.rem(y + 1 + i, side)
+
+    def tri_copy(w, n, p):
+        vector, chip_core = ((c, mine), (o, other))[w]
+        return rdma(trial_bf.at[vector], trial_all.at[c, own_cols], tri_s.at[w, n], tri_r.at[c, b], chip_core, p)
+
+    def tri_out(w, n):
+        return tri_copy(w, n, (facing, beside(0), beside(1), beside(2), b)[n])
+
+    tri_order = [(0, 0), (1, 0), (0, 1), (0, 2), (0, 3), (1, 1), (1, 2), (1, 3), (1, 4)]
+    for w, n in tri_order[:5]:
+        tri_out(w, n).start()
     loads[2].wait()
     send_vir = rdma(vir.at[c], vir.at[c], x_s.at[0], x_r.at[0], other, b)
     send_occ = rdma(occ.at[c], occ.at[c], x_s.at[1], x_r.at[1], other, b)
     send_vir.start()
     send_occ.start()
-    each(bands, lambda i: tri_cross(i).start())
+    for w, n in tri_order[5:]:
+        tri_out(w, n).start()
     trial_all[c, own_cols, :] = trial_bf[c]
+
+    def landed(dst, recv):
+        rdma(dst, dst, x_s.at[0], recv, mine, b).wait_recv()
+
+    def tri_piece(s, p):
+        return trial_all.at[s, block(p * width, width)]
+
+    def tri_landed(s, p):
+        landed(tri_piece(s, p), tri_r.at[s, p])
+
+    def tri_pass(s, i):
+        return rdma(
+            tri_piece(s, facing), tri_piece(s, facing), tri_f.at[s, i], tri_r.at[s, facing], mine, beside(i)
+        )
+
+    for s in (c, o):
+        tri_landed(s, facing)
+        for i in range(side - 1):
+            tri_pass(s, i).start()
 
     def occ1_wait(i):
         @pl.when((i != z) | (y != z))
@@ -187,22 +217,10 @@
     def occ_yx(row, i):
         return x_send(part_b(quarter, row), fx_s.at[row, i], fx_r.at[quarter, row], i)
 
-    def landed(dst, recv):
-        rdma(dst, dst, x_s.at[0], recv, mine, b).wait_recv()
-
     each(3, lambda i: occ_x(i).start())
     each(side - 1, lambda i: occ_y(i).start())
 
     vir_t[c] = vir[c].T
-
-    def tri_wait_same(i):
-        p = band_peer(i)
-        part = block(p * width, width)
-        rdma(trial_bf.at[c], trial_all.at[c, part], tri_s.at[0, i], tri_r.at[c, p], mine, p).wait_recv()
-
-    def tri_wait_cross(i):
-        part = block(i * width, width)
-        rdma(trial_bf.at[o], trial_all.at[o, part], tri_s.at[1, i], tri_r.at[o, i], other, i).wait_recv()
 
     def t_copy(s, i):
         return rdma(t_mine.at[h, s], t_all.at[2 * j + s], t_s.at[s, i], t_r.at[s, j], 2 * deep(i) + c, b)
@@ -230,12 +248,18 @@
         t_cross(s).start()
         each(depth - 1, lambda i: t_copy(s, i).start())
 
-    each(bands - 1, tri_wait_same)
+    def tri_rest(s):
+        for i in range(side - 1):
+            tri_landed(s, beside(i))
+            tri_landed(s, behind(i))
+
+    tri_rest(c)
     local = t_make(c)
     t_start(c)
     rdma(vir.at[c], vir.at[o], x_s.at[0], x_r.at[0], other, b).wait_recv()
     rdma(occ.at[c], occ.at[o], x_s.at[1], x_r.at[1], other, b).wait_recv()
-    each(bands, tri_wait_cross)
+    tri_rest(o)
+    tri_landed(o, b)
     local = local + t_make(o)
 
     high = local.astype(BF)
@@ -354,13 +378,13 @@
     loads[5].wait()
 
     tile = 16
-    fours = 4
+    group = 2
 
     def u_copy(dest, s):
         return rdma(u_send.at[2 * dest + s], u_recv.at[j, s], u_s.at[s, dest], u_r.at[s, j], 2 * dest + c, b)
 
     def screen(g, s):
-        dests = [j ^ (chips - 1 - fours * g - n) for n in range(fours)]
+        dests = [j ^ (chips - 1 - group * g - n) for n in range(group)]
 
         def rows_step(r):
             part = block(r * tile, tile)
@@ -376,23 +400,25 @@
             left = jnp.dot(s_bf[n, :, :rows], points_of(dest, s, 0), preferred_element_type=F32)
             sums.append(left + jnp.dot(s_bf[n, :, rows:], points_of(dest, s, 1), preferred_element_type=F32))
         for n, dest in enumerate(dests):
-            u_send[2 * dest + s] = sums[n].astype(BF)
-        for n, dest in enumerate(dests):
-            if chips - 1 - fours * g - n:
+            if chips - 1 - group * g - n:
+                u_send[2 * dest + s] = sums[n].astype(BF)
                 u_copy(dest, s).start()
+            else:
+                u_recv[j, s] = sums[n].astype(BF)
 
     def finish(s):
-        mine_rows = block(h * half, half)
-        acc_w[s, mine_rows, :] = acc_w[s, mine_rows, :] - u_send[2 * j + s].astype(F32)
-
-        def u_arrived(i):
+        def u_landed(i):
             p = chip_peer(i)
-            rdma(u_send.at[2 * p + s], u_recv.at[p, s], u_s.at[s, p], u_r.at[s, p], 2 * p + c, b).wait_recv()
-            part = block((p // depth) * half, half)
-            acc_w[s, part, :] = acc_w[s, part, :] - u_recv[p, s].astype(F32)
-
-        each(chips - 1, u_arrived)
-        sig_send[s] = jnp.dot(vir_t[s], acc_w[s].astype(BF), preferred_element_type=F32).astype(BF)
+            landed(u_recv.at[p, s], u_r.at[s, p])
+
+        each(chips - 1, u_landed)
+        sides = []
+        for e in range(2):
+            total = u_recv[e * depth, s].astype(F32)
+            for p in range(1, depth):
+                total = total + u_recv[e * depth + p, s].astype(F32)
+            sides.append((acc_w[s, e * half : (e + 1) * half, :] - total).astype(BF))
+        sig_send[s] = jnp.dot(vir_t[s], jnp.concatenate(sides, axis=0), preferred_element_type=F32).astype(BF)
 
         def sig_start(p):
             @pl.when((c != s) | (p != b))
@@ -410,11 +436,10 @@
             sig_send.at[s, block(p * width, width)], sig_recv.at[c, b], g_s.at[s, p], g_r.at[c, b], 2 * j + s, p
         )
 
-    screen(0, 0)
-    screen(1, 0)
-    screen(0, 1)
-
-    screen(1, 1)
+    for s in range(2):
+        for g in range(chips // group):
+            screen(g, s)
+
     def d2_wait(i):
         p = band_peer(i)
         rdma(dens2.at[p], dens2.at[p], d2_s.at[i], d2_r.at[p], mine, p).wait_recv()
@@ -430,8 +455,11 @@
         acc_w[s] = pot * occ[s].astype(F32)
 
     finish(0)
-    each(bands - 1, lambda i: tri_same(i).wait_send())
-    each(bands, lambda i: tri_cross(i).wait_send())
+    for w, n in tri_order:
+        tri_out(w, n).wait_send()
+    for s in range(2):
+        for i in range(side - 1):
+            tri_pass(s, i).wait_send()
 
     def occ1_sent(i):
         @pl.when((i != y) | (y != z))
@@ -499,6 +527,7 @@
         turned = jnp.transpose(trial[0], (0, 2, 1))
         far = pl.BlockSpec(memory_space=pltpu.HBM)
         dma = pltpu.SemaphoreType.DMA
+        operands = (minus, turned, occ[0], vir[0], coulomb, exch, occ_energy, vir_energy)
         result = pl.pallas_call(
             kernel,
             out_shape=jax.ShapeDtypeStruct((2, width, nocc), F32),
@@ -520,7 +549,7 @@
                 pltpu.VMEM((2, 4, chips // 2, bands // 2, 2 * rows // bands, nocc), BF),
                 pltpu.VMEM((nk, half, cols), BF),
                 pltpu.VMEM((nk, half, cols), BF),
-                pltpu.VMEM((4, half, cols), BF),
+                pltpu.VMEM((2, half, cols), BF),
                 pltpu.VMEM((nk, half, nocc), BF),
                 pltpu.VMEM((chips, 2, half, nocc), BF),
                 pltpu.VMEM((2, rows, nocc), F32),
@@ -529,7 +558,7 @@
                 pltpu.VMEM((rows, aux), BF),
                 pltpu.VMEM((2, nvir, nocc), BF),
                 pltpu.VMEM((2, bands, width, nocc), BF),
-                dma((2, bands)), dma((2, bands)),
+                dma((2, 5)), dma((2, bands)), dma((2, 3)),
                 dma((2,)), dma((2,)),
                 dma((bands // 2,)), dma((chips // 2,)),
                 dma((3,)), dma((4,)),
@@ -545,10 +574,10 @@
                 dma((9,)),
             ],
             compiler_params=pltpu.CompilerParams(
-                collective_id=0, has_side_effects=True, vmem_limit_bytes=67043328
+                collective_id=0, has_side_effects=True, vmem_limit_bytes=48 * 1024 * 1024
             ),
             name="sigma",
-        )(minus, turned, occ[0], vir[0], coulomb, exch, occ_energy, vir_energy)
+        )(*[pltpu.with_memory_space_constraint(a, pltpu.HBM) for a in operands])
         return jnp.transpose(result, (0, 2, 1))[None]
 
     in_specs = (

time: 49.4 us -> 46.6 us (0.943)
  Pallas kernels: 47.6 us -> 45.8 us
  local copies, waits for them, and re-layouts: 1.55 us -> 0.65 us
    pallas_call x1, Pallas kernels: 47.6 us -> 45.8 us  [per_device(): pl.pallas_call(kernel, out_shape=jax.ShapeDtypeStruct((2, width, nocc), F...]
    unnamed x1, local copies, waits for them, and re-layouts: 1.55 us -> 0.65 us
where the time goes in v6:
time: 46.6 us; the launch traced here: 46.5 us
  Pallas kernels  45.8 us (98%)
  local copies, waits for them, and re-layouts  0.65 us (1%)
    pallas_call x1, Pallas kernels, per_device(): pl.pallas_call(kernel, out_shape=jax.ShapeDtypeStruct((2, width, nocc), F...  45.8 us

profile of v6, /device:TPU:1, one launch (start us, length us, event | category | flops | bytes accessed | tf_op | source)
XLA Modules:
  0.0 46.5 jit_solution(3297802493655647574)
XLA Ops:
  0.0 45.8 %sigma.1 = f32[2,112,128]{2,1,0:T(8,128)S(1)} custom-call(s32[16,16]{1,0:T(8,128)} %minus_h.1, f32[2,112,128]{2,1,0:T(8,128)} %bitcast.10, bf16[256,128]{1,0:T(8,128)(2,1)} %bitcast.11, bf16[256,896]{1,0:T(8,128)(2,1)} %bitcast.9, bf16[256,2048]{1,0:T(8,128)(2,1)} %coulomb.1, bf16[16,256,2048]{2,1,0:T(8,128)(2,1)} %exch.1, f32[1,128]{1,0:T(1,128)} %occ_e_h.1, ...), custom_call_target="tpu_custom_call" | custom-call | tf_op jit(solution)/shard_map/sigma/pallas_call | solution.py:531
  45.8 0.6 %copy.10 = f32[1,2,128,112]{2,3,1,0:T(8,128)} copy(f32[1,2,128,112]{2,3,1,0:T(8,128)S(1)} %bitcast.8) | data formatting | bytes 229376

commit v7 on v6

--- a/solution.py
+++ b/solution.py
@@ -357,34 +357,37 @@
     def points_of(p, s, e):
         return occ_c[s, 2 * (p // depth) + e, lax.rem(p, depth)].reshape(rows, nocc)
 
-    def pairs_of(s):
-        for p in range(chips):
+    def pairs_of(s, column):
+        for n in range(depth):
+            p = column * depth + n
             for e in range(2):
                 pairs[2 * p + s, :, e * rows : (e + 1) * rows] = lax.dot_general(
                     t_all[2 * p + s], points_of(p, s, e), ALONG, preferred_element_type=F32
                 ).astype(BF)
 
-    pairs_of(c)
+    pairs_of(c, h)
+    pairs_of(c, 1 - h)
 
     def occ3_wait(n):
         q = quarter ^ (n // 2)
         landed(occ_c.at[o, q, pl.ds(lax.rem(n, 2) * (depth // 2), depth // 2)], o3_r.at[n])
 
-    each(8, occ3_wait)
-
-    pairs_of(o)
+    each(4, occ3_wait)
+    pairs_of(o, h)
+    each(4, lambda n: occ3_wait(n + 4))
+
+    pairs_of(o, 1 - h)
     loads[3].wait()
     loads[4].wait()
     loads[5].wait()
 
     tile = 16
-    group = 2
 
     def u_copy(dest, s):
         return rdma(u_send.at[2 * dest + s], u_recv.at[j, s], u_s.at[s, dest], u_r.at[s, j], 2 * dest + c, b)
 
-    def screen(g, s):
-        dests = [j ^ (chips - 1 - group * g - n) for n in range(group)]
+    def screen(offsets, s):
+        dests = [j ^ m for m in offsets]
 
         def rows_step(r):
             part = block(r * tile, tile)
@@ -400,7 +403,7 @@
             left = jnp.dot(s_bf[n, :, :rows], points_of(dest, s, 0), preferred_element_type=F32)
             sums.append(left + jnp.dot(s_bf[n, :, rows:], points_of(dest, s, 1), preferred_element_type=F32))
         for n, dest in enumerate(dests):
-            if chips - 1 - group * g - n:
+            if offsets[n]:
                 u_send[2 * dest + s] = sums[n].astype(BF)
                 u_copy(dest, s).start()
             else:
@@ -420,16 +423,16 @@
             sides.append((acc_w[s, e * half : (e + 1) * half, :] - total).astype(BF))
         sig_send[s] = jnp.dot(vir_t[s], jnp.concatenate(sides, axis=0), preferred_element_type=F32).astype(BF)
 
-        def sig_start(p):
-            @pl.when((c != s) | (p != b))
-            def _():
-                sig_copy(s, p).start()
-
-        each(bands, sig_start)
+        for n in range(bands - 1, 0, -1):
+            sig_copy(s, b ^ n).start()
 
         @pl.when(c == s)
         def _():
             sig_recv[c, b] = sig_send[s, own_cols, :]
+
+        @pl.when(c != s)
+        def _():
+            sig_copy(s, b).start()
 
     def sig_copy(s, p):
         return rdma(
@@ -437,8 +440,8 @@
         )
 
     for s in range(2):
-        for g in range(chips // group):
-            screen(g, s)
+        for m in range(depth - 1, -1, -1):
+            screen((depth + m, m), s)
 
     def d2_wait(i):
         p = band_peer(i)
@@ -549,7 +552,7 @@
                 pltpu.VMEM((2, 4, chips // 2, bands // 2, 2 * rows // bands, nocc), BF),
                 pltpu.VMEM((nk, half, cols), BF),
                 pltpu.VMEM((nk, half, cols), BF),
-                pltpu.VMEM((2, half, cols), BF),
+                pltpu.VMEM((4, half, cols), BF),
                 pltpu.VMEM((nk, half, nocc), BF),
                 pltpu.VMEM((chips, 2, half, nocc), BF),
                 pltpu.VMEM((2, rows, nocc), F32),

time: 46.6 us -> 45.9 us (0.985)
  Pallas kernels: 45.8 us -> 45.1 us
    pallas_call x1, Pallas kernels: 45.8 us -> 45.1 us  [per_device(): pl.pallas_call(kernel, out_shape=jax.ShapeDtypeStruct((2, width, nocc), F...]
where the time goes in v7:
time: 45.9 us; the launch traced here: 45.8 us
  Pallas kernels  45.1 us (98%)
  local copies, waits for them, and re-layouts  0.65 us (1%)
    pallas_call x1, Pallas kernels, per_device(): pl.pallas_call(kernel, out_shape=jax.ShapeDtypeStruct((2, width, nocc), F...  45.1 us

profile of v7, /device:TPU:1, one launch (start us, length us, event | category | flops | bytes accessed | tf_op | source)
XLA Modules:
  0.0 45.8 jit_solution(13373381144714712165)
XLA Ops:
  0.0 45.1 %sigma.1 = f32[2,112,128]{2,1,0:T(8,128)S(1)} custom-call(s32[16,16]{1,0:T(8,128)} %minus_h.1, f32[2,112,128]{2,1,0:T(8,128)} %bitcast.10, bf16[256,128]{1,0:T(8,128)(2,1)} %bitcast.11, bf16[256,896]{1,0:T(8,128)(2,1)} %bitcast.9, bf16[256,2048]{1,0:T(8,128)(2,1)} %coulomb.1, bf16[16,256,2048]{2,1,0:T(8,128)(2,1)} %exch.1, f32[1,128]{1,0:T(1,128)} %occ_e_h.1, ...), custom_call_target="tpu_custom_call" | custom-call | tf_op jit(solution)/shard_map/sigma/pallas_call | solution.py:534
  45.1 0.6 %copy.10 = f32[1,2,128,112]{2,3,1,0:T(8,128)} copy(f32[1,2,128,112]{2,3,1,0:T(8,128)S(1)} %bitcast.8) | data formatting | bytes 229376

commit v8 on v7

--- a/solution.py
+++ b/solution.py
@@ -189,9 +189,6 @@
 
     each(depth, occ1_wait)
 
-    def piece(q, row):
-        return occ_c.at[c, q, :, row]
-
     def part_a(q, row):
         return occ_c.at[c, q, pl.ds(0, depth // 2), row]
 
@@ -205,11 +202,13 @@
     def y_send(src, send, recv, i):
         return rdma(src, src, send, recv, mine, xl * side + lax.rem(y + 1 + i, side))
 
-    def occ_x(i):
-        return x_send(piece(quarter, y), ox_s.at[i], ox_r.at[quarter], i)
-
-    def occ_y(i):
-        return y_send(piece(quarter, y), oy_s.at[i], oy_r.at[y], i)
+    parts = (part_a, part_b)
+
+    def occ_x(n, i):
+        return x_send(parts[n](quarter, y), ox_s.at[n, i], ox_r.at[n, quarter], i)
+
+    def occ_y(n, i):
+        return y_send(parts[n](quarter, y), oy_s.at[n, i], oy_r.at[n, y], i)
 
     def occ_xy(q, i):
         return y_send(part_a(q, y), fy_s.at[q, i], fy_r.at[q, y], i)
@@ -217,8 +216,9 @@
     def occ_yx(row, i):
         return x_send(part_b(quarter, row), fx_s.at[row, i], fx_r.at[quarter, row], i)
 
-    each(3, lambda i: occ_x(i).start())
-    each(side - 1, lambda i: occ_y(i).start())
+    for n in range(2):
+        each(3, lambda i: occ_x(n, i).start())
+        each(side - 1, lambda i: occ_y(1 - n, i).start())
 
     vir_t[c] = vir[c].T
 
@@ -277,16 +277,20 @@
 
     def x_arrived(i):
         q = quarter ^ (i + 1)
-        landed(piece(q, y), ox_r.at[q])
+        landed(part_a(q, y), ox_r.at[0, q])
         each(side - 1, lambda n: occ_xy(q, n).start())
 
     def y_arrived(i):
         row = lax.rem(y + 1 + i, side)
-        landed(piece(quarter, row), oy_r.at[row])
+        landed(part_b(quarter, row), oy_r.at[1, row])
         each(3, lambda n: occ_yx(row, n).start())
 
     each(3, x_arrived)
     each(side - 1, y_arrived)
+
+    def second_halves(i):
+        row = lax.rem(y + 1 + i, side)
+        landed(part_a(quarter, row), oy_r.at[0, row])
 
     def t_pass(s):
         t_landed(s, partner)
@@ -300,6 +304,7 @@
         there = occ_c.at[c, q, pl.ds(lax.rem(n, 2) * (depth // 2), depth // 2)]
         return rdma(there, there, o3_s.at[n], o3_r.at[n], other, b)
 
+    each(side - 1, second_halves)
     occ3(0).start()
     occ3(1).start()
 
@@ -326,6 +331,7 @@
         each(side - 1, from_y)
         occ3(2 * i + 2).start()
         each(side - 1, from_x)
+        landed(part_b(q, y), ox_r.at[1, q])
         occ3(2 * i + 3).start()
 
     each(3, occ_rest)
@@ -472,8 +478,9 @@
     each(side, occ1_sent)
     send_vir.wait_send()
     send_occ.wait_send()
-    each(3, lambda i: occ_x(i).wait_send())
-    each(side - 1, lambda i: occ_y(i).wait_send())
+    for n in range(2):
+        each(3, lambda i: occ_x(n, i).wait_send())
+        each(side - 1, lambda i: occ_y(n, i).wait_send())
 
     def forwarded(i):
         each(side - 1, lambda n: occ_xy(quarter ^ (i + 1), n).wait_send())
@@ -490,6 +497,18 @@
 
     finish(1)
 
+    def sig_sent(s):
+        for n in range(1, bands):
+            sig_copy(s, b ^ n).wait_send()
+
+        @pl.when(c != s)
+        def _():
+            sig_copy(s, b).wait_send()
+
+    for s in range(2):
+        each(chips - 1, lambda i: u_copy(chip_peer(i), s).wait_send())
+    sig_sent(0)
+
     def sig_wait_same(i):
         p = band_peer(i)
         rdma(sig_send.at[0, own_cols], sig_recv.at[c, p], g_s.at[0, i], g_r.at[c, p], mine, p).wait_recv()
@@ -505,15 +524,7 @@
             sums = sums + sig_recv[v, p].astype(F32)
         out[v] = out[v] + sums
 
-    for s in range(2):
-        each(chips - 1, lambda i: u_copy(chip_peer(i), s).wait_send())
-
-        def sig_sent(p):
-            @pl.when((c != s) | (p != b))
-            def _():
-                sig_copy(s, p).wait_send()
-
-        each(bands, sig_sent)
+    sig_sent(1)
 
 
 def solution(mesh):
@@ -564,8 +575,8 @@
                 dma((2, 5)), dma((2, bands)), dma((2, 3)),
                 dma((2,)), dma((2,)),
                 dma((bands // 2,)), dma((chips // 2,)),
-                dma((3,)), dma((4,)),
-                dma((3,)), dma((bands // 2,)),
+                dma((2, 3)), dma((2, 4)),
+                dma((2, 3)), dma((2, bands // 2)),
                 dma((4, 3)), dma((4, bands // 2)),
                 dma((bands // 2, 3)), dma((4, bands // 2)),
                 dma((8,)), dma((8,)),

time: 45.9 us -> 44.9 us (0.978)
  Pallas kernels: 45.1 us -> 44.2 us
    pallas_call x1, Pallas kernels: 45.1 us -> 44.2 us  [per_device(): pl.pallas_call(kernel, out_shape=jax.ShapeDtypeStruct((2, width, nocc), F...]
where the time goes in v8:
time: 44.9 us; the launch traced here: 44.8 us
  Pallas kernels  44.2 us (98%)
  local copies, waits for them, and re-layouts  0.65 us (1%)
    pallas_call x1, Pallas kernels, per_device(): pl.pallas_call(kernel, out_shape=jax.ShapeDtypeStruct((2, width, nocc), F...  44.2 us

profile of v8, /device:TPU:1, one launch (start us, length us, event | category | flops | bytes accessed | tf_op | source)
XLA Modules:
  0.0 44.8 jit_solution(6997427610504025436)
XLA Ops:
  0.0 44.2 %sigma.1 = f32[2,112,128]{2,1,0:T(8,128)S(1)} custom-call(s32[16,16]{1,0:T(8,128)} %minus_h.1, f32[2,112,128]{2,1,0:T(8,128)} %bitcast.10, bf16[256,128]{1,0:T(8,128)(2,1)} %bitcast.11, bf16[256,896]{1,0:T(8,128)(2,1)} %bitcast.9, bf16[256,2048]{1,0:T(8,128)(2,1)} %coulomb.1, bf16[16,256,2048]{2,1,0:T(8,128)(2,1)} %exch.1, f32[1,128]{1,0:T(1,128)} %occ_e_h.1, ...), custom_call_target="tpu_custom_call" | custom-call | tf_op jit(solution)/shard_map/sigma/pallas_call | solution.py:545
  44.2 0.6 %copy.10 = f32[1,2,128,112]{2,3,1,0:T(8,128)} copy(f32[1,2,128,112]{2,3,1,0:T(8,128)S(1)} %bitcast.8) | data formatting | bytes 229376

commit v9 on v8

--- a/solution.py
+++ b/solution.py
@@ -396,14 +396,16 @@
         dests = [j ^ m for m in offsets]
 
         def rows_step(r):
-            part = block(r * tile, tile)
-            for n, dest in enumerate(dests):
-                acc = jnp.zeros((tile, cols), F32)
-                for q in range(nk):
-                    acc = acc + pairs[minus[2 * dest + s, q], part, :].astype(F32) * k_bf[q, part, :].astype(F32)
-                s_bf[n, part, :] = acc.astype(BF)
-
-        each(half // tile, rows_step)
+            for t in range(2):
+                part = block((r * 2 + t) * tile, tile)
+                for n, dest in enumerate(dests):
+                    acc = jnp.zeros((tile, cols), F32)
+                    for q in range(nk):
+                        source = minus[2 * dest + s, q]
+                        acc = acc + pairs[source, part, :].astype(F32) * k_bf[q, part, :].astype(F32)
+                    s_bf[n, part, :] = acc.astype(BF)
+
+        each(half // tile // 2, rows_step)
         sums = []
         for n, dest in enumerate(dests):
             left = jnp.dot(s_bf[n, :, :rows], points_of(dest, s, 0), preferred_element_type=F32)
@@ -427,10 +429,14 @@
             for p in range(1, depth):
                 total = total + u_recv[e * depth + p, s].astype(F32)
             sides.append((acc_w[s, e * half : (e + 1) * half, :] - total).astype(BF))
-        sig_send[s] = jnp.dot(vir_t[s], jnp.concatenate(sides, axis=0), preferred_element_type=F32).astype(BF)
-
-        for n in range(bands - 1, 0, -1):
-            sig_copy(s, b ^ n).start()
+        weight = jnp.concatenate(sides, axis=0)
+        for column in (1 - xl, xl):
+            part = block(column * side * width, side * width)
+            sig_send[s, part, :] = jnp.dot(vir_t[s, part, :], weight, preferred_element_type=F32).astype(BF)
+            for n in range(side - 1, -1, -1):
+                if column is xl and n == 0:
+                    continue
+                sig_copy(s, column * side + (y ^ n)).start()
 
         @pl.when(c == s)
         def _():

time: 44.9 us -> 44.6 us (level)
  no operation moved by 1% of the time
where the time goes in v9:
time: 44.6 us; the launch traced here: 44.5 us
  Pallas kernels  43.8 us (98%)
  local copies, waits for them, and re-layouts  0.65 us (1%)
    pallas_call x1, Pallas kernels, per_device(): pl.pallas_call(kernel, out_shape=jax.ShapeDtypeStruct((2, width, nocc), F...  43.8 us

profile of v9, /device:TPU:1, one launch (start us, length us, event | category | flops | bytes accessed | tf_op | source)
XLA Modules:
  0.0 44.5 jit_solution(17394119819585028419)
XLA Ops:
  0.0 43.8 %sigma.1 = f32[2,112,128]{2,1,0:T(8,128)S(1)} custom-call(s32[16,16]{1,0:T(8,128)} %minus_h.1, f32[2,112,128]{2,1,0:T(8,128)} %bitcast.10, bf16[256,128]{1,0:T(8,128)(2,1)} %bitcast.11, bf16[256,896]{1,0:T(8,128)(2,1)} %bitcast.9, bf16[256,2048]{1,0:T(8,128)(2,1)} %coulomb.1, bf16[16,256,2048]{2,1,0:T(8,128)(2,1)} %exch.1, f32[1,128]{1,0:T(1,128)} %occ_e_h.1, ...), custom_call_target="tpu_custom_call" | custom-call | tf_op jit(solution)/shard_map/sigma/pallas_call | solution.py:551
  43.8 0.6 %copy.10 = f32[1,2,128,112]{2,3,1,0:T(8,128)} copy(f32[1,2,128,112]{2,3,1,0:T(8,128)S(1)} %bitcast.8) | data formatting | bytes 229376

commit v10 on v9

--- a/solution.py
+++ b/solution.py
@@ -238,15 +238,18 @@
         landed(t_all.at[2 * p + s], t_r.at[s, p])
 
     def t_make(s):
-        value = jnp.dot(vir[s], trial_all[s], preferred_element_type=F32)
-        t_mine[0, s] = value[:half].astype(BF)
-        t_mine[1, s] = value[half:].astype(BF)
-        t_all[2 * j + s] = t_mine[h, s]
-        return occ[s].astype(F32) * value
-
-    def t_start(s):
-        t_cross(s).start()
-        each(depth - 1, lambda i: t_copy(s, i).start())
+        products = []
+        for e in (1 - h, h):
+            part = block(e * half, half)
+            value = jnp.dot(vir[s, part, :], trial_all[s], preferred_element_type=F32)
+            t_mine[e, s] = value.astype(BF)
+            if e is h:
+                each(depth - 1, lambda i: t_copy(s, i).start())
+                t_all[2 * j + s] = t_mine[h, s]
+            else:
+                t_cross(s).start()
+            products.append(occ[s, part, :].astype(F32) * value)
+        return products
 
     def tri_rest(s):
         for i in range(side - 1):
@@ -255,25 +258,24 @@
 
     tri_rest(c)
     local = t_make(c)
-    t_start(c)
     rdma(vir.at[c], vir.at[o], x_s.at[0], x_r.at[0], other, b).wait_recv()
     rdma(occ.at[c], occ.at[o], x_s.at[1], x_r.at[1], other, b).wait_recv()
     tri_rest(o)
     tri_landed(o, b)
-    local = local + t_make(o)
-
-    high = local.astype(BF)
-    low = (local - high.astype(F32)).astype(BF)
+    local = [left + right for left, right in zip(local, t_make(o))]
+
     ones = jnp.ones((8, nocc), BF)
-    dens1[j] = lax.dot_general(ones, high, ALONG, preferred_element_type=F32) + lax.dot_general(
-        ones, low, ALONG, preferred_element_type=F32
-    )
+    for e, products in zip((1 - h, h), local):
+        high = products.astype(BF)
+        low = (products - high.astype(F32)).astype(BF)
+        dens1[j, :, block(e * half, half, 128)] = lax.dot_general(
+            ones, high, ALONG, preferred_element_type=F32
+        ) + lax.dot_general(ones, low, ALONG, preferred_element_type=F32)
 
     def d1_copy(i):
         return rdma(dens1.at[j], dens1.at[j], d1_s.at[i], d1_r.at[j], 2 * chip_peer(i) + c, b)
 
     each(chips - 1, lambda i: d1_copy(i).start())
-    t_start(o)
 
     def x_arrived(i):
         q = quarter ^ (i + 1)
@@ -297,7 +299,6 @@
         each(depth - 1, lambda i: t_forward(s, i).start())
 
     t_pass(c)
-    t_pass(o)
 
     def occ3(n):
         q = quarter ^ (n // 2)
@@ -307,6 +308,7 @@
     each(side - 1, second_halves)
     occ3(0).start()
     occ3(1).start()
+    t_pass(o)
 
     vir_t[o] = vir[o].T
     turn[...] = jnp.zeros_like(turn)

time: 44.6 us -> 44.5 us (level)
  no operation moved by 1% of the time
where the time goes in v10:
time: 44.5 us; the launch traced here: 44.4 us
  Pallas kernels  43.8 us (98%)
  local copies, waits for them, and re-layouts  0.65 us (1%)
    pallas_call x1, Pallas kernels, per_device(): pl.pallas_call(kernel, out_shape=jax.ShapeDtypeStruct((2, width, nocc), F...  43.8 us

profile of v10, /device:TPU:1, one launch (start us, length us, event | category | flops | bytes accessed | tf_op | source)
XLA Modules:
  0.0 44.4 jit_solution(13172228361729354656)
XLA Ops:
  0.0 43.8 %sigma.1 = f32[2,112,128]{2,1,0:T(8,128)S(1)} custom-call(s32[16,16]{1,0:T(8,128)} %minus_h.1, f32[2,112,128]{2,1,0:T(8,128)} %bitcast.10, bf16[256,128]{1,0:T(8,128)(2,1)} %bitcast.11, bf16[256,896]{1,0:T(8,128)(2,1)} %bitcast.9, bf16[256,2048]{1,0:T(8,128)(2,1)} %coulomb.1, bf16[16,256,2048]{2,1,0:T(8,128)(2,1)} %exch.1, f32[1,128]{1,0:T(1,128)} %occ_e_h.1, ...), custom_call_target="tpu_custom_call" | custom-call | tf_op jit(solution)/shard_map/sigma/pallas_call | solution.py:553
  43.8 0.6 %copy.10 = f32[1,2,128,112]{2,3,1,0:T(8,128)} copy(f32[1,2,128,112]{2,3,1,0:T(8,128)S(1)} %bitcast.8) | data formatting | bytes 229376
